TPU v7x, 32 devices: a whole 2x2x4 slice. The times are simulated.
32 devices in a mesh: stage: 4 (over z), tp: 8 (over y, x, core).
Axes of the slice: x: 2, y: 2, z: 4, core: 2. Of those that a mesh axis runs over, the one named last changes fastest.
Arguments:
- x: bfloat16 [8, 2048, 1024], P(None, 'tp')
- g: bfloat16 [4, 2, 1024], P('stage')
- w1: bfloat16 [4, 2, 1024, 4096], P('stage', None, None, 'tp')
- w2: bfloat16 [4, 2, 4096, 1024], P('stage', None, 'tp')
Outputs:
- output: bfloat16 [4, 8, 2048, 1024], P('stage', None, 'tp')
All inputs are finite; a program needn't handle non-finite values.
Results may differ from a plain program's by a relative error of at most 0.02.
Values are sent between devices in bfloat16 or wider.
A program may use at most 1 GiB of HBM per device.

v0:
```python
import jax
import jax.numpy as jnp
from jax import lax
from jax.sharding import PartitionSpec as P

EPS = 1e-5


def _ln(y, g):
    yf = y.astype(jnp.float32)
    mu = jnp.mean(yf, axis=-1, keepdims=True)
    var = jnp.mean(jnp.square(yf - mu), axis=-1, keepdims=True)
    return ((yf - mu) * lax.rsqrt(var + EPS) * g.astype(jnp.float32)).astype(jnp.bfloat16)


def _block(y, g, w1, w2):
    h = lax.all_gather(_ln(y, g), 'tp', axis=0, tiled=True)
    a = jax.nn.gelu(jnp.dot(h, w1, preferred_element_type=jnp.float32)).astype(jnp.bfloat16)
    p = jnp.dot(a, w2, preferred_element_type=jnp.float32).astype(jnp.bfloat16)
    r = lax.psum_scatter(p, 'tp', scatter_dimension=0, tiled=True)
    return (y.astype(jnp.float32) + r.astype(jnp.float32)).astype(jnp.bfloat16)


def solution(mesh):
    S = mesh.shape['stage']
    fwd = [(i, i + 1) for i in range(S - 1)]

    def local(x, g, w1, w2):
        s = lax.axis_index('stage')
        M = x.shape[0]
        nb = g.shape[1]
        out = jnp.zeros_like(x)
        recv = jnp.zeros_like(x[0])
        for k in range(M + S - 1):
            y = jnp.where(s == 0, x[min(k, M - 1)], recv)
            for b in range(nb):
                y = _block(y, g[0, b], w1[0, b], w2[0, b])
            m = k - s
            mc = jnp.clip(m, 0, M - 1)
            old = lax.dynamic_index_in_dim(out, mc, 0, keepdims=False)
            out = lax.dynamic_update_index_in_dim(out, jnp.where((m >= 0) & (m < M), y, old), mc, 0)
            if k < M + S - 2:
                recv = lax.ppermute(y, 'stage', fwd)
        return out[None]

    return jax.shard_map(
        local, mesh=mesh,
        in_specs=(P(None, 'tp', None), P('stage', None, None),
                  P('stage', None, None, 'tp'), P('stage', None, 'tp', None)),
        out_specs=P('stage', None, 'tp', None), check_vma=False)
```

profile of v0, /device:TPU:24, one launch (start us, length us, event | category | flops | bytes accessed | tf_op | source)
XLA Modules:
  0.0 2392.0 jit_solution(5349668231176617979)
XLA Ops:
  12.0 37.4 %all-gather.23.cloned.1.call-done = bf16[2048,1024]{1,0:T(8,128)(2,1)} async-done(((bf16[256,1024]{1,0:T(8,128)(2,1)}), bf16[2048,1024]{1,0:T(8,128)(2,1)}) %all-gather.23.cloned.1.call-update) | async-done | bytes 4194320 | tf_op jit(solution)/shard_map/all_gather | solution.py:17
  59.4 50.9 %reduce-scatter.23.cloned.1.call-done = bf16[256,1024]{1,0:T(8,128)(2,1)} async-done(((bf16[2048,1024]{1,0:T(8,128)(2,1)}), bf16[256,1024]{1,0:T(8,128)(2,1)}) %reduce-scatter.23.cloned.1.call-update) | async-done | bytes 524304 | tf_op jit(solution)/shard_map/reduce_scatter | solution.py:20
  113.2 36.4 %all-gather.25.cloned.1.call-done = bf16[2048,1024]{1,0:T(8,128)(2,1)} async-done(((bf16[256,1024]{1,0:T(8,128)(2,1)}), bf16[2048,1024]{1,0:T(8,128)(2,1)}) %all-gather.25.cloned.1.call-update) | async-done | bytes 4194320 | tf_op jit(solution)/shard_map/all_gather | solution.py:17
  159.4 50.9 %reduce-scatter.25.cloned.1.call-done = bf16[256,1024]{1,0:T(8,128)(2,1)} async-done(((bf16[2048,1024]{1,0:T(8,128)(2,1)}), bf16[256,1024]{1,0:T(8,128)(2,1)}) %reduce-scatter.25.cloned.1.call-update) | async-done | bytes 524304 | tf_op jit(solution)/shard_map/reduce_scatter | solution.py:20
  278.0 50.9 %reduce-scatter.27.cloned.1.call-done = bf16[256,1024]{1,0:T(8,128)(2,1)} async-done(((bf16[2048,1024]{1,0:T(8,128)(2,1)}), bf16[256,1024]{1,0:T(8,128)(2,1)}) %reduce-scatter.27.cloned.1.call-update) | async-done | bytes 524304 | tf_op jit(solution)/shard_map/reduce_scatter | solution.py:20
  379.0 49.8 %reduce-scatter.29.cloned.1.call-done = bf16[256,1024]{1,0:T(8,128)(2,1)} async-done(((bf16[2048,1024]{1,0:T(8,128)(2,1)}), bf16[256,1024]{1,0:T(8,128)(2,1)}) %reduce-scatter.29.cloned.1.call-update) | async-done | bytes 524304 | tf_op jit(solution)/shard_map/reduce_scatter | solution.py:20
  495.2 50.9 %reduce-scatter.31.cloned.1.call-done = bf16[256,1024]{1,0:T(8,128)(2,1)} async-done(((bf16[2048,1024]{1,0:T(8,128)(2,1)}), bf16[256,1024]{1,0:T(8,128)(2,1)}) %reduce-scatter.31.cloned.1.call-update) | async-done | bytes 524304 | tf_op jit(solution)/shard_map/reduce_scatter | solution.py:20
  596.1 49.8 %reduce-scatter.33.cloned.1.call-done = bf16[256,1024]{1,0:T(8,128)(2,1)} async-done(((bf16[2048,1024]{1,0:T(8,128)(2,1)}), bf16[256,1024]{1,0:T(8,128)(2,1)}) %reduce-scatter.33.cloned.1.call-update) | async-done | bytes 524304 | tf_op jit(solution)/shard_map/reduce_scatter | solution.py:20
  712.2 50.9 %reduce-scatter.35.cloned.1.call-done = bf16[256,1024]{1,0:T(8,128)(2,1)} async-done(((bf16[2048,1024]{1,0:T(8,128)(2,1)}), bf16[256,1024]{1,0:T(8,128)(2,1)}) %reduce-scatter.35.cloned.1.call-update) | async-done | bytes 524304 | tf_op jit(solution)/shard_map/reduce_scatter | solution.py:20
  813.2 49.8 %reduce-scatter.37.cloned.1.call-done = bf16[256,1024]{1,0:T(8,128)(2,1)} async-done(((bf16[2048,1024]{1,0:T(8,128)(2,1)}), bf16[256,1024]{1,0:T(8,128)(2,1)}) %reduce-scatter.37.cloned.1.call-update) | async-done | bytes 524304 | tf_op jit(solution)/shard_map/reduce_scatter | solution.py:20
  929.4 50.9 %reduce-scatter.39.cloned.1.call-done = bf16[256,1024]{1,0:T(8,128)(2,1)} async-done(((bf16[2048,1024]{1,0:T(8,128)(2,1)}), bf16[256,1024]{1,0:T(8,128)(2,1)}) %reduce-scatter.39.cloned.1.call-update) | async-done | bytes 524304 | tf_op jit(solution)/shard_map/reduce_scatter | solution.py:20
  1030.3 49.8 %reduce-scatter.41.cloned.1.call-done = bf16[256,1024]{1,0:T(8,128)(2,1)} async-done(((bf16[2048,1024]{1,0:T(8,128)(2,1)}), bf16[256,1024]{1,0:T(8,128)(2,1)}) %reduce-scatter.41.cloned.1.call-update) | async-done | bytes 524304 | tf_op jit(solution)/shard_map/reduce_scatter | solution.py:20
  1146.5 50.9 %reduce-scatter.43.cloned.1.call-done = bf16[256,1024]{1,0:T(8,128)(2,1)} async-done(((bf16[2048,1024]{1,0:T(8,128)(2,1)}), bf16[256,1024]{1,0:T(8,128)(2,1)}) %reduce-scatter.43.cloned.1.call-update) | async-done | bytes 524304 | tf_op jit(solution)/shard_map/reduce_scatter | solution.py:20
  1247.4 49.8 %reduce-scatter.45.cloned.1.call-done = bf16[256,1024]{1,0:T(8,128)(2,1)} async-done(((bf16[2048,1024]{1,0:T(8,128)(2,1)}), bf16[256,1024]{1,0:T(8,128)(2,1)}) %reduce-scatter.45.cloned.1.call-update) | async-done | bytes 524304 | tf_op jit(solution)/shard_map/reduce_scatter | solution.py:20
  1363.7 50.9 %reduce-scatter.47.cloned.1.call-done = bf16[256,1024]{1,0:T(8,128)(2,1)} async-done(((bf16[2048,1024]{1,0:T(8,128)(2,1)}), bf16[256,1024]{1,0:T(8,128)(2,1)}) %reduce-scatter.47.cloned.1.call-update) | async-done | bytes 524304 | tf_op jit(solution)/shard_map/reduce_scatter | solution.py:20
  1464.6 49.8 %reduce-scatter.49.cloned.1.call-done = bf16[256,1024]{1,0:T(8,128)(2,1)} async-done(((bf16[2048,1024]{1,0:T(8,128)(2,1)}), bf16[256,1024]{1,0:T(8,128)(2,1)}) %reduce-scatter.49.cloned.1.call-update) | async-done | bytes 524304 | tf_op jit(solution)/shard_map/reduce_scatter | solution.py:20
  1580.8 50.9 %reduce-scatter.51.cloned.1.call-done = bf16[256,1024]{1,0:T(8,128)(2,1)} async-done(((bf16[2048,1024]{1,0:T(8,128)(2,1)}), bf16[256,1024]{1,0:T(8,128)(2,1)}) %reduce-scatter.51.cloned.1.call-update) | async-done | bytes 524304 | tf_op jit(solution)/shard_map/reduce_scatter | solution.py:20
  1681.7 49.8 %reduce-scatter.53.cloned.1.call-done = bf16[256,1024]{1,0:T(8,128)(2,1)} async-done(((bf16[2048,1024]{1,0:T(8,128)(2,1)}), bf16[256,1024]{1,0:T(8,128)(2,1)}) %reduce-scatter.53.cloned.1.call-update) | async-done | bytes 524304 | tf_op jit(solution)/shard_map/reduce_scatter | solution.py:20
  1797.9 50.9 %reduce-scatter.55.cloned.1.call-done = bf16[256,1024]{1,0:T(8,128)(2,1)} async-done(((bf16[2048,1024]{1,0:T(8,128)(2,1)}), bf16[256,1024]{1,0:T(8,128)(2,1)}) %reduce-scatter.55.cloned.1.call-update) | async-done | bytes 524304 | tf_op jit(solution)/shard_map/reduce_scatter | solution.py:20
  1898.8 49.8 %reduce-scatter.57.cloned.1.call-done = bf16[256,1024]{1,0:T(8,128)(2,1)} async-done(((bf16[2048,1024]{1,0:T(8,128)(2,1)}), bf16[256,1024]{1,0:T(8,128)(2,1)}) %reduce-scatter.57.cloned.1.call-update) | async-done | bytes 524304 | tf_op jit(solution)/shard_map/reduce_scatter | solution.py:20
  2015.0 50.9 %reduce-scatter.59.cloned.1.call-done = bf16[256,1024]{1,0:T(8,128)(2,1)} async-done(((bf16[2048,1024]{1,0:T(8,128)(2,1)}), bf16[256,1024]{1,0:T(8,128)(2,1)}) %reduce-scatter.59.cloned.1.call-update) | async-done | bytes 524304 | tf_op jit(solution)/shard_map/reduce_scatter | solution.py:20
  2115.9 49.8 %reduce-scatter.61.cloned.1.call-done = bf16[256,1024]{1,0:T(8,128)(2,1)} async-done(((bf16[2048,1024]{1,0:T(8,128)(2,1)}), bf16[256,1024]{1,0:T(8,128)(2,1)}) %reduce-scatter.61.cloned.1.call-update) | async-done | bytes 524304 | tf_op jit(solution)/shard_map/reduce_scatter | solution.py:20
  2232.1 50.9 %reduce-scatter.63.cloned.1.call-done = bf16[256,1024]{1,0:T(8,128)(2,1)} async-done(((bf16[2048,1024]{1,0:T(8,128)(2,1)}), bf16[256,1024]{1,0:T(8,128)(2,1)}) %reduce-scatter.63.cloned.1.call-update) | async-done | bytes 524304 | tf_op jit(solution)/shard_map/reduce_scatter | solution.py:20
  2336.5 46.3 %reduce-scatter.65.cloned.1.call-done = bf16[256,1024]{1,0:T(8,128)(2,1)} async-done(((bf16[2048,1024]{1,0:T(8,128)(2,1)}), bf16[256,1024]{1,0:T(8,128)(2,1)}) %reduce-scatter.65.cloned.1.call-update) | async-done | bytes 524304 | tf_op jit(solution)/shard_map/reduce_scatter | solution.py:20
  (287 shorter events, 1198.7 us)
Async XLA Ops:
  11.9 98.3 %reduce-scatter.23.cloned.1.call-start = ((), (), s32[]{:S(2)}) async-start(), calls=%async_computation.23 | async-start | bytes 4718592 | tf_op jit(solution)/shard_map/reduce_scatter | solution.py:20
  113.2 97.1 %reduce-scatter.25.cloned.1.call-start = ((), (), s32[]{:S(2)}) async-start(), calls=%async_computation.25 | async-start | bytes 4718592 | tf_op jit(solution)/shard_map/reduce_scatter | solution.py:20
  159.4 108.9 %all-gather.27.cloned.1.call-start = ((), (), s32[]{:S(2)}) async-start(), calls=%async_computation.26 | async-start | bytes 4718592 | tf_op jit(solution)/shard_map/all_gather | solution.py:17
  231.8 97.1 %reduce-scatter.27.cloned.1.call-start = ((), (), s32[]{:S(2)}) async-start(), calls=%async_computation.27 | async-start | bytes 4718592 | tf_op jit(solution)/shard_map/reduce_scatter | solution.py:20
  331.6 97.1 %reduce-scatter.29.cloned.1.call-start = ((), (), s32[]{:S(2)}) async-start(), calls=%async_computation.29 | async-start | bytes 4718592 | tf_op jit(solution)/shard_map/reduce_scatter | solution.py:20
  377.8 107.6 %all-gather.31.cloned.1.call-start = ((), (), s32[]{:S(2)}) async-start(), calls=%async_computation.30 | async-start | bytes 4718592 | tf_op jit(solution)/shard_map/all_gather | solution.py:17
  448.9 97.1 %reduce-scatter.31.cloned.1.call-start = ((), (), s32[]{:S(2)}) async-start(), calls=%async_computation.31 | async-start | bytes 4718592 | tf_op jit(solution)/shard_map/reduce_scatter | solution.py:20
  594.9 107.5 %all-gather.35.cloned.1.call-start = ((), (), s32[]{:S(2)}) async-start(), calls=%async_computation.34 | async-start | bytes 4718592 | tf_op jit(solution)/shard_map/all_gather | solution.py:17
  666.0 97.1 %reduce-scatter.35.cloned.1.call-start = ((), (), s32[]{:S(2)}) async-start(), calls=%async_computation.35 | async-start | bytes 4718592 | tf_op jit(solution)/shard_map/reduce_scatter | solution.py:20
  765.8 97.1 %reduce-scatter.37.cloned.1.call-start = ((), (), s32[]{:S(2)}) async-start(), calls=%async_computation.37 | async-start | bytes 4718592 | tf_op jit(solution)/shard_map/reduce_scatter | solution.py:20
  812.0 107.6 %all-gather.39.cloned.1.call-start = ((), (), s32[]{:S(2)}) async-start(), calls=%async_computation.38 | async-start | bytes 4718592 | tf_op jit(solution)/shard_map/all_gather | solution.py:17
  883.2 97.1 %reduce-scatter.39.cloned.1.call-start = ((), (), s32[]{:S(2)}) async-start(), calls=%async_computation.39 | async-start | bytes 4718592 | tf_op jit(solution)/shard_map/reduce_scatter | solution.py:20
  983.0 97.1 %reduce-scatter.41.cloned.1.call-start = ((), (), s32[]{:S(2)}) async-start(), calls=%async_computation.41 | async-start | bytes 4718592 | tf_op jit(solution)/shard_map/reduce_scatter | solution.py:20
  1029.2 107.6 %all-gather.43.cloned.1.call-start = ((), (), s32[]{:S(2)}) async-start(), calls=%async_computation.42 | async-start | bytes 4718592 | tf_op jit(solution)/shard_map/all_gather | solution.py:17
  1200.1 97.1 %reduce-scatter.45.cloned.1.call-start = ((), (), s32[]{:S(2)}) async-start(), calls=%async_computation.45 | async-start | bytes 4718592 | tf_op jit(solution)/shard_map/reduce_scatter | solution.py:20
  1246.3 107.6 %all-gather.47.cloned.1.call-start = ((), (), s32[]{:S(2)}) async-start(), calls=%async_computation.46 | async-start | bytes 4718592 | tf_op jit(solution)/shard_map/all_gather | solution.py:17
  1317.4 97.1 %reduce-scatter.47.cloned.1.call-start = ((), (), s32[]{:S(2)}) async-start(), calls=%async_computation.47 | async-start | bytes 4718592 | tf_op jit(solution)/shard_map/reduce_scatter | solution.py:20
  1463.4 107.6 %all-gather.51.cloned.1.call-start = ((), (), s32[]{:S(2)}) async-start(), calls=%async_computation.50 | async-start | bytes 4718592 | tf_op jit(solution)/shard_map/all_gather | solution.py:17
  1680.6 107.6 %all-gather.55.cloned.1.call-start = ((), (), s32[]{:S(2)}) async-start(), calls=%async_computation.54 | async-start | bytes 4718592 | tf_op jit(solution)/shard_map/all_gather | solution.py:17
  1851.5 97.1 %reduce-scatter.57.cloned.1.call-start = ((), (), s32[]{:S(2)}) async-start(), calls=%async_computation.57 | async-start | bytes 4718592 | tf_op jit(solution)/shard_map/reduce_scatter | solution.py:20
  1897.6 107.6 %all-gather.59.cloned.1.call-start = ((), (), s32[]{:S(2)}) async-start(), calls=%async_computation.58 | async-start | bytes 4718592 | tf_op jit(solution)/shard_map/all_gather | solution.py:17
  2068.6 97.1 %reduce-scatter.61.cloned.1.call-start = ((), (), s32[]{:S(2)}) async-start(), calls=%async_computation.61 | async-start | bytes 4718592 | tf_op jit(solution)/shard_map/reduce_scatter | solution.py:20
  2114.8 107.6 %all-gather.63.cloned.1.call-start = ((), (), s32[]{:S(2)}) async-start(), calls=%async_computation.62 | async-start | bytes 4718592 | tf_op jit(solution)/shard_map/all_gather | solution.py:17
  2185.9 97.1 %reduce-scatter.63.cloned.1.call-start = ((), (), s32[]{:S(2)}) async-start(), calls=%async_computation.63 | async-start | bytes 4718592 | tf_op jit(solution)/shard_map/reduce_scatter | solution.py:20
  (32 other events, 2056.7 us)
Sparse Core Ops, SparseCore 0:
  12.1 37.2 all-gather.22
  59.5 50.7 reduce-scatter.22
  113.3 36.3 all-gather.24
  159.5 50.7 reduce-scatter.24
  278.1 50.7 reduce-scatter.26
  377.9 50.7 reduce-scatter.28
  495.2 50.7 reduce-scatter.30
  595.0 50.7 reduce-scatter.32
  712.3 50.7 reduce-scatter.34
  812.1 50.7 reduce-scatter.36
  929.4 50.7 reduce-scatter.38
  1029.3 50.7 reduce-scatter.40
  1146.6 50.7 reduce-scatter.42
  1246.4 50.7 reduce-scatter.44
  1363.7 50.7 reduce-scatter.46
  1463.6 50.7 reduce-scatter.48
  1580.8 50.7 reduce-scatter.50
  1680.7 50.7 reduce-scatter.52
  1798.0 50.7 reduce-scatter.54
  1897.8 50.7 reduce-scatter.56
  2015.1 50.7 reduce-scatter.58
  2114.9 50.7 reduce-scatter.60
  2232.2 50.7 reduce-scatter.62
  2331.9 50.7 reduce-scatter.64
  (20 shorter events, 724.8 us)
where the time goes:
time: 2400 us; the launch traced here: 2390 us
  waiting for transfers between devices  2050 us (85%)
  matrix products  214 us (9%)
  other arithmetic  84.7 us (4%)
    reduce_scatter x22, waiting for transfers between devices, _block(): r = lax.psum_scatter(p, 'tp', scatter_dimension=0, tiled=True)  1100 us
    all_gather x22, waiting for transfers between devices, _block(): h = lax.all_gather(_ln(y, g), 'tp', axis=0, tiled=True)  800 us
    dot_general x22, matrix products, _block(): p = jnp.dot(a, w2, preferred_element_type=jnp.float32).astype(jnp.bfloat16)  214 us
    ppermute x10, waiting for transfers between devices, local(): recv = lax.ppermute(y, 'stage', fwd)  140 us
  transfers between devices with their start and end apart: 54, of which 54 were waited for; matrix products, arithmetic and copies ran while one was open for 1% of the time, Pallas kernels for 0%

commit v1 on v0

v1 whole, which is shorter than its diff:
```python
import jax
import jax.numpy as jnp
from jax import lax
from jax.sharding import PartitionSpec as P

EPS = 1e-5


def _ln(y, g):
    yf = y.astype(jnp.float32)
    mu = jnp.mean(yf, axis=-1, keepdims=True)
    var = jnp.mean(jnp.square(yf - mu), axis=-1, keepdims=True)
    return ((yf - mu) * lax.rsqrt(var + EPS) * g.astype(jnp.float32)).astype(jnp.bfloat16)


def _block(y, g, w1, w2):
    h = _ln(y, g)
    a = jax.nn.gelu(jnp.dot(h, w1, preferred_element_type=jnp.float32)).astype(jnp.bfloat16)
    r = jnp.dot(a, w2, preferred_element_type=jnp.float32)
    return (y.astype(jnp.float32) + r).astype(jnp.bfloat16)


def solution(mesh):
    S = mesh.shape['stage']
    fwd = [(i, i + 1) for i in range(S - 1)]
    lag = 2

    def local(x, g, w1, w2):
        s = lax.axis_index('stage')
        M = x.shape[0]
        nb = g.shape[1]
        full1 = [lax.all_gather(w1[0, b], 'tp', axis=1, tiled=True) for b in range(nb)]
        full2 = [lax.all_gather(w2[0, b], 'tp', axis=0, tiled=True) for b in range(nb)]
        steps = M + lag * (S - 1)
        outs, sent = [], []
        for k in range(steps):
            xin = x[min(k, M - 1)]
            y = jnp.where(s == 0, xin, sent[k - lag]) if k >= lag else xin
            for b in range(nb):
                y = _block(y, g[0, b], full1[b], full2[b])
            outs.append(y)
            if k < steps - lag:
                sent.append(lax.ppermute(y, 'stage', fwd))
        out = lax.dynamic_slice_in_dim(jnp.stack(outs), lag * s, M, axis=0)
        return out[None]

    return jax.shard_map(
        local, mesh=mesh,
        in_specs=(P(None, 'tp', None), P('stage', None, None),
                  P('stage', None, None, 'tp'), P('stage', None, 'tp', None)),
        out_specs=P('stage', None, 'tp', None), check_vma=False)
```

time: 2400 us -> 666 us (0.28)
  the two profiles are of different devices: /device:TPU:24 before, /device:TPU:0 now
where the time goes in v1:
time: 666 us; the launch traced here: 656 us
  matrix products  310 us (47%)
  waiting for transfers between devices  251 us (38%)
  starting transfers between devices  45.6 us (7%)
  other arithmetic  22 us (3%)
  between operations  13.9 us (2%)
  local copies, waits for them, and re-layouts  13.5 us (2%)
    dot_general x28, matrix products, _block(): r = jnp.dot(a, w2, preferred_element_type=jnp.float32)  310 us
    all_gather x2, waiting for transfers between devices, local(): lax.all_gather(w2[0, b], 'tp', axis=0, tiled=True)  111 us
    all_gather x2, waiting for transfers between devices, local(): lax.all_gather(w1[0, b], 'tp', axis=1, tiled=True)  87.3 us
    ppermute x12, waiting for transfers between devices, local(): sent.append(lax.ppermute(y, 'stage', fwd))  50.9 us
    ppermute x12, starting transfers between devices, local(): sent.append(lax.ppermute(y, 'stage', fwd))  45.5 us
  transfers between devices with their start and end apart: 16, of which 11 were waited for; matrix products, arithmetic and copies ran while one was open for 17% of the time, Pallas kernels for 0%

profile of v1, /device:TPU:0, one launch (start us, length us, event | category | flops | bytes accessed | tf_op | source)
XLA Modules:
  0.0 655.9 jit_solution(440192232664492766)
XLA Ops:
  15.7 52.4 %all-gather.9.cloned.1.call-done = bf16[1,1,1024,4096]{3,2,1,0:T(8,128)(2,1)} async-done(((bf16[1,1,1024,512]{3,2,1,0:T(8,128)(2,1)}), bf16[1,1,1024,4096]{3,2,1,0:T(8,128)(2,1)}) %all-gather.9.cloned.1.call-update) | async-done | bytes 8388624 | tf_op jit(solution)/shard_map/all_gather | solution.py:32
  68.1 55.8 %all-gather.11.cloned.1.call-done = bf16[1,1,4096,1024]{3,2,1,0:T(8,128)(2,1)} async-done(((bf16[1,1,512,1024]{3,2,1,0:T(8,128)(2,1)}), bf16[1,1,4096,1024]{3,2,1,0:T(8,128)(2,1)}) %all-gather.11.cloned.1.call-update) | async-done | bytes 8388624 | tf_op jit(solution)/shard_map/all_gather | solution.py:33
  123.9 11.0 %convert_reduce_fusion.24 = (f32[256]{0:T(256)S(1)}, bf16[256,1024]{1,0:T(8,128)(2,1)S(1)}) fusion(bf16[1,1,4096,1024]{3,2,1,0:T(8,128)(2,1)} %all-gather.11.cloned.1.call-done, bf16[1,1,1024,4096]{3,2,1,0:T(8,128)(2,1)} %all-gather.9.cloned.1.call-done, f32[256]{0:T(256)S(1)} %add_rsqrt_fusion.25, f32[256]{0:T(256)S(1)} %get-tuple-element.89, ...), kind=kOutput, calls=%fused_computation.439 | convolution fusion | flops 4307025920 | bytes 18357248 | tf_op jit(solution)/shard_map/dot_general | solution.py:19
  135.2 11.0 %convert_reduce_fusion.25 = (f32[256]{0:T(256)S(1)}, bf16[256,1024]{1,0:T(8,128)(2,1)S(1)}) fusion(bf16[1,1,4096,1024]{3,2,1,0:T(8,128)(2,1)} %all-gather.11.cloned.1.call-done, bf16[1,1,1024,4096]{3,2,1,0:T(8,128)(2,1)} %all-gather.9.cloned.1.call-done, f32[1024]{0:T(1024)S(1)} %bitcast.613, f32[256]{0:T(256)S(1)} %add_rsqrt_fusion.27, ...), kind=kOutput, calls=%fused_computation.442 | convolution fusion | flops 4307025920 | bytes 18357248 | tf_op jit(solution)/shard_map/dot_general | solution.py:19
  146.5 34.8 %all-gather.13.cloned.1.call-done = bf16[1,1,1024,4096]{3,2,1,0:T(8,128)(2,1)} async-done(((bf16[1,1,1024,512]{3,2,1,0:T(8,128)(2,1)}), bf16[1,1,1024,4096]{3,2,1,0:T(8,128)(2,1)}) %all-gather.13.cloned.1.call-update) | async-done | bytes 8388624 | tf_op jit(solution)/shard_map/all_gather | solution.py:32
  181.3 55.7 %all-gather.15.cloned.1.call-done = bf16[1,1,4096,1024]{3,2,1,0:T(8,128)(2,1)} async-done(((bf16[1,1,512,1024]{3,2,1,0:T(8,128)(2,1)}), bf16[1,1,4096,1024]{3,2,1,0:T(8,128)(2,1)}) %all-gather.15.cloned.1.call-update) | async-done | bytes 8388624 | tf_op jit(solution)/shard_map/all_gather | solution.py:33
  237.0 11.7 %bitcast_dynamic-update-slice_fusion.11 = (bf16[14,256,1024]{2,1,0:T(8,128)(2,1)}, bf16[256,1024]{1,0:T(8,128)(2,1)S(1)}) fusion(bf16[1,1,4096,1024]{3,2,1,0:T(8,128)(2,1)} %all-gather.15.cloned.1.call-done, bf16[1,1,1024,4096]{3,2,1,0:T(8,128)(2,1)} %all-gather.13.cloned.1.call-done, bf16[256,1024]{1,0:T(8,128)(2,1)S(1)} %get-tuple-element.48, ...), kind=kOutput, calls=%fused_computation.646 | convolution fusion | flops 4306501632 | bytes 18880512 | tf_op jit(solution)/shard_map/dot_general | solution.py:19
  248.7 11.5 %bitcast_dynamic-update-slice_fusion.10 = (bf16[14,256,1024]{2,1,0:T(8,128)(2,1)}, bf16[256,1024]{1,0:T(8,128)(2,1)S(1)}) fusion(bf16[14,256,1024]{2,1,0:T(8,128)(2,1)} %get-tuple-element.49, bf16[1,1,4096,1024]{3,2,1,0:T(8,128)(2,1)} %all-gather.15.cloned.1.call-done, bf16[1,1,1024,4096]{3,2,1,0:T(8,128)(2,1)} %all-gather.13.cloned.1.call-done, ...), kind=kOutput, calls=%fused_computation.645 | convolution fusion | flops 4306501632 | bytes 18880512 | tf_op jit(solution)/shard_map/dot_general | solution.py:19
  263.6 11.5 %collective-permute-done.1 = bf16[256,1024]{1,0:T(8,128)(2,1)S(1)} collective-permute-done((bf16[256,1024]{1,0:T(8,128)(2,1)S(1)}, bf16[256,1024]{1,0:T(8,128)(2,1)S(1)}, u32[]{:S(2)}, u32[]{:S(2)}) %collective-permute-start.1) | collective-permute-done | bytes 524320 | tf_op jit(solution)/shard_map/ppermute | solution.py:43
  276.7 10.8 %convert_reduce_fusion.20 = (f32[256]{0:T(256)S(1)}, bf16[256,1024]{1,0:T(8,128)(2,1)S(1)}) fusion(bf16[1,1,4096,1024]{3,2,1,0:T(8,128)(2,1)} %all-gather.11.cloned.1.call-done, bf16[1,1,1024,4096]{3,2,1,0:T(8,128)(2,1)} %all-gather.9.cloned.1.call-done, bf16[256,1024]{1,0:T(8,128)(2,1)S(1)} %get-tuple-element.30, f32[256]{0:T(256)S(1)} %add_rsqrt_fusion.21, ...), kind=kOutput, calls=%fused_computation.427 | convolution fusion | flops 4307025920 | bytes 17832960 | tf_op jit(solution)/shard_map/dot_general | solution.py:19
  364.6 10.8 %convert_reduce_fusion.12 = (f32[256]{0:T(256)S(1)}, bf16[256,1024]{1,0:T(8,128)(2,1)S(1)}) fusion(bf16[1,1,4096,1024]{3,2,1,0:T(8,128)(2,1)} %all-gather.11.cloned.1.call-done, bf16[1,1,1024,4096]{3,2,1,0:T(8,128)(2,1)} %all-gather.9.cloned.1.call-done, bf16[256,1024]{1,0:T(8,128)(2,1)S(1)} %get-tuple-element.22, f32[256]{0:T(256)S(1)} %add_rsqrt_fusion.13, ...), kind=kOutput, calls=%fused_computation.403 | convolution fusion | flops 4307025920 | bytes 17832960 | tf_op jit(solution)/shard_map/dot_general | solution.py:19
  375.8 11.1 %fusion.553 = bf16[256,1024]{1,0:T(8,128)(2,1)S(1)} fusion(bf16[1,1,4096,1024]{3,2,1,0:T(8,128)(2,1)} %all-gather.15.cloned.1.call-done, bf16[256,1024]{1,0:T(8,128)(2,1)S(1)} %get-tuple-element.64, bf16[1,1,1024,4096]{3,2,1,0:T(8,128)(2,1)} %all-gather.13.cloned.1.call-done, f32[256]{0:T(256)S(1)} %add_rsqrt_fusion.12, ...), kind=kOutput, calls=%fused_computation.466 | convolution fusion | flops 4306501632 | bytes 17831936 | tf_op jit(solution)/shard_map/dot_general | solution.py:19
  391.3 11.5 %bitcast_dynamic-update-slice_fusion.9 = (bf16[14,256,1024]{2,1,0:T(8,128)(2,1)}, bf16[256,1024]{1,0:T(8,128)(2,1)S(1)}) fusion(bf16[14,256,1024]{2,1,0:T(8,128)(2,1)} %get-tuple-element.53, bf16[1,1,4096,1024]{3,2,1,0:T(8,128)(2,1)} %all-gather.15.cloned.1.call-done, bf16[1,1,1024,4096]{3,2,1,0:T(8,128)(2,1)} %all-gather.13.cloned.1.call-done, ...), kind=kOutput, calls=%fused_computation.643 | convolution fusion | flops 4306501632 | bytes 18880512 | tf_op jit(solution)/shard_map/dot_general | solution.py:19
  437.7 11.9 %bitcast_dynamic-update-slice_fusion.7 = (bf16[14,256,1024]{2,1,0:T(8,128)(2,1)}, bf16[256,1024]{1,0:T(8,128)(2,1)}) fusion(bf16[14,256,1024]{2,1,0:T(8,128)(2,1)} %bitcast_dynamic-update-slice_fusion.8, bf16[1,1,4096,1024]{3,2,1,0:T(8,128)(2,1)} %all-gather.15.cloned.1.call-done, bf16[1,1,1024,4096]{3,2,1,0:T(8,128)(2,1)} %all-gather.13.cloned.1.call-done, ...), kind=kOutput, calls=%fused_computation.639 | convolution fusion | flops 4306501632 | bytes 18880512 | tf_op jit(solution)/shard_map/dot_general | solution.py:19
  470.8 10.8 %convert_reduce_fusion.14 = (f32[256]{0:T(256)S(1)}, bf16[256,1024]{1,0:T(8,128)(2,1)S(1)}) fusion(bf16[1,1,4096,1024]{3,2,1,0:T(8,128)(2,1)} %all-gather.11.cloned.1.call-done, bf16[1,1,1024,4096]{3,2,1,0:T(8,128)(2,1)} %all-gather.9.cloned.1.call-done, bf16[256,1024]{1,0:T(8,128)(2,1)S(1)} %get-tuple-element.24, f32[256]{0:T(256)S(1)} %add_rsqrt_fusion.15, ...), kind=kOutput, calls=%fused_computation.409 | convolution fusion | flops 4307025920 | bytes 17832960 | tf_op jit(solution)/shard_map/dot_general | solution.py:19
  481.9 11.5 %bitcast_dynamic-update-slice_fusion.5 = (bf16[14,256,1024]{2,1,0:T(8,128)(2,1)}, bf16[256,1024]{1,0:T(8,128)(2,1)S(1)}) fusion(bf16[14,256,1024]{2,1,0:T(8,128)(2,1)} %bitcast_dynamic-update-slice_fusion.6, bf16[1,1,4096,1024]{3,2,1,0:T(8,128)(2,1)} %all-gather.15.cloned.1.call-done, bf16[1,1,1024,4096]{3,2,1,0:T(8,128)(2,1)} %all-gather.13.cloned.1.call-done, ...), kind=kOutput, calls=%fused_computation.635 | convolution fusion | flops 4306501632 | bytes 18880512 | tf_op jit(solution)/shard_map/dot_general | solution.py:19
  504.0 10.8 %convert_reduce_fusion.10 = (f32[256]{0:T(256)S(1)}, bf16[256,1024]{1,0:T(8,128)(2,1)S(1)}) fusion(bf16[1,1,4096,1024]{3,2,1,0:T(8,128)(2,1)} %all-gather.11.cloned.1.call-done, bf16[1,1,1024,4096]{3,2,1,0:T(8,128)(2,1)} %all-gather.9.cloned.1.call-done, bf16[256,1024]{1,0:T(8,128)(2,1)S(1)} %get-tuple-element.36, f32[256]{0:T(256)S(1)} %add_rsqrt_fusion.11, ...), kind=kOutput, calls=%fused_computation.397 | convolution fusion | flops 4307025920 | bytes 17832960 | tf_op jit(solution)/shard_map/dot_general | solution.py:19
  515.4 10.8 %convert_reduce_fusion.4 = (f32[256]{0:T(256)S(1)}, bf16[256,1024]{1,0:T(8,128)(2,1)S(1)}) fusion(bf16[1,1,4096,1024]{3,2,1,0:T(8,128)(2,1)} %all-gather.11.cloned.1.call-done, bf16[1,1,1024,4096]{3,2,1,0:T(8,128)(2,1)} %all-gather.9.cloned.1.call-done, bf16[256,1024]{1,0:T(8,128)(2,1)S(1)} %get-tuple-element.14, f32[256]{0:T(256)S(1)} %add_rsqrt_fusion.5, ...), kind=kOutput, calls=%fused_computation.379 | convolution fusion | flops 4307025920 | bytes 17832960 | tf_op jit(solution)/shard_map/dot_general | solution.py:19
  526.5 10.9 %fusion.577 = bf16[256,1024]{1,0:T(8,128)(2,1)S(1)} fusion(bf16[1,1,4096,1024]{3,2,1,0:T(8,128)(2,1)} %all-gather.15.cloned.1.call-done, bf16[256,1024]{1,0:T(8,128)(2,1)S(1)} %get-tuple-element.80, bf16[1,1,1024,4096]{3,2,1,0:T(8,128)(2,1)} %all-gather.13.cloned.1.call-done, f32[256]{0:T(256)S(1)} %add_rsqrt_fusion.4, ...), kind=kOutput, calls=%fused_computation.474 | convolution fusion | flops 4306501632 | bytes 17831936 | tf_op jit(solution)/shard_map/dot_general | solution.py:19
  541.8 11.5 %bitcast_dynamic-update-slice_fusion.3 = (bf16[14,256,1024]{2,1,0:T(8,128)(2,1)}, bf16[256,1024]{1,0:T(8,128)(2,1)S(1)}) fusion(bf16[14,256,1024]{2,1,0:T(8,128)(2,1)} %bitcast_dynamic-update-slice_fusion.4, bf16[1,1,4096,1024]{3,2,1,0:T(8,128)(2,1)} %all-gather.15.cloned.1.call-done, bf16[1,1,1024,4096]{3,2,1,0:T(8,128)(2,1)} %all-gather.13.cloned.1.call-done, ...), kind=kOutput, calls=%fused_computation.626 | convolution fusion | flops 4306501632 | bytes 18880512 | tf_op jit(solution)/shard_map/dot_general | solution.py:19
  585.9 11.7 %bitcast_dynamic-update-slice_fusion.1 = (bf16[14,256,1024]{2,1,0:T(8,128)(2,1)}, bf16[256,1024]{1,0:T(8,128)(2,1)S(1)}) fusion(bf16[14,256,1024]{2,1,0:T(8,128)(2,1)} %bitcast_dynamic-update-slice_fusion.2, bf16[1,1,4096,1024]{3,2,1,0:T(8,128)(2,1)} %all-gather.15.cloned.1.call-done, bf16[1,1,1024,4096]{3,2,1,0:T(8,128)(2,1)} %all-gather.13.cloned.1.call-done, ...), kind=kOutput, calls=%fused_computation.624 | convolution fusion | flops 4306501632 | bytes 18880512 | tf_op jit(solution)/shard_map/dot_general | solution.py:19
  610.2 10.8 %convert_reduce_fusion.2 = (f32[256]{0:T(256)S(1)}, bf16[256,1024]{1,0:T(8,128)(2,1)S(1)}) fusion(bf16[1,1,4096,1024]{3,2,1,0:T(8,128)(2,1)} %all-gather.11.cloned.1.call-done, bf16[1,1,1024,4096]{3,2,1,0:T(8,128)(2,1)} %all-gather.9.cloned.1.call-done, bf16[256,1024]{1,0:T(8,128)(2,1)S(1)} %get-tuple-element.12, f32[256]{0:T(256)S(1)} %add_rsqrt_fusion.3, ...), kind=kOutput, calls=%fused_computation.373 | convolution fusion | flops 4307025920 | bytes 17832960 | tf_op jit(solution)/shard_map/dot_general | solution.py:19
  621.3 11.5 %fusion.657 = bf16[14,256,1024]{2,1,0:T(8,128)(2,1)} fusion(bf16[14,256,1024]{2,1,0:T(8,128)(2,1)} %bitcast_dynamic-update-slice_fusion, bf16[1,1,4096,1024]{3,2,1,0:T(8,128)(2,1)} %all-gather.15.cloned.1.call-done, bf16[256,1024]{1,0:T(8,128)(2,1)S(1)} %get-tuple-element.86, bf16[1,1,1024,4096]{3,2,1,0:T(8,128)(2,1)} %all-gather.13.cloned.1.call-done, ...), kind=kOutput, calls=%fused_computation.538 | convolution fusion | flops 4306501632 | bytes 18356224 | tf_op jit(solution)/shard_map/dot_general | solution.py:19
  632.9 11.5 %fusion.651 = bf16[14,256,1024]{2,1,0:T(8,128)(2,1)} fusion(bf16[14,256,1024]{2,1,0:T(8,128)(2,1)} %fusion.657, bf16[1,1,4096,1024]{3,2,1,0:T(8,128)(2,1)} %all-gather.15.cloned.1.call-done, bf16[256,1024]{1,0:T(8,128)(2,1)S(1)} %get-tuple-element.88, bf16[1,1,1024,4096]{3,2,1,0:T(8,128)(2,1)} %all-gather.13.cloned.1.call-done, f32[256]{0:T(256)S(1)} %add_rsqrt_fusion, ...), kind=kOutput, calls=%fused_computation.536 | convolution fusion | flops 4306501632 | bytes 18356224 | tf_op jit(solution)/shard_map/dot_general | solution.py:19
  (144 shorter events, 218.6 us)
Async XLA Ops:
  6.5 3.2 copy-start
  6.5 61.6 %all-gather.9.cloned.1.call-start = ((), (), s32[]{:S(2)}) async-start(), calls=%async_computation | async-start | bytes 9437184 | tf_op jit(solution)/shard_map/all_gather | solution.py:32
  9.7 6.0 copy-start.1
  9.7 114.2 %all-gather.11.cloned.1.call-start = ((), (), s32[]{:S(2)}) async-start(), calls=%async_computation.1 | async-start | bytes 9437184 | tf_op jit(solution)/shard_map/all_gather | solution.py:33
  11.3 170.0 %all-gather.13.cloned.1.call-start = ((), (), s32[]{:S(2)}) async-start(), calls=%async_computation.2 | async-start | bytes 9437184 | tf_op jit(solution)/shard_map/all_gather | solution.py:32
  12.0 225.0 %all-gather.15.cloned.1.call-start = ((), (), s32[]{:S(2)}) async-start(), calls=%async_computation.3 | async-start | bytes 9437184 | tf_op jit(solution)/shard_map/all_gather | solution.py:33
  260.2 14.9 %collective-permute-start.1 = (bf16[256,1024]{1,0:T(8,128)(2,1)S(1)}, bf16[256,1024]{1,0:T(8,128)(2,1)S(1)}, u32[]{:S(2)}, u32[]{:S(2)}) collective-permute-start(bf16[256,1024]{1,0:T(8,128)(2,1)S(1)} %get-tuple-element.54), channel_id=1, source_target_pairs={{0,8},{8,16},{16,24},{1,9},{9,17},{17,25},{2,10},{10,18},{18,26},{... | collective-permute-start | bytes 1572872 | tf_op jit(solution)/shard_map/ppermute | solution.py:43
  298.5 16.7 %collective-permute-start.3 = (bf16[256,1024]{1,0:T(8,128)(2,1)S(1)}, bf16[256,1024]{1,0:T(8,128)(2,1)S(1)}, u32[]{:S(2)}, u32[]{:S(2)}) collective-permute-start(bf16[256,1024]{1,0:T(8,128)(2,1)S(1)} %fusion.529), channel_id=1, source_target_pairs={{0,8},{8,16},{16,24},{1,9},{9,17},{17,25},{2,10},{10,18},{18,26},{... | collective-permute-start | bytes 1572872 | tf_op jit(solution)/shard_map/ppermute | solution.py:43
  303.0 40.3 %collective-permute-start = (bf16[256,1024]{1,0:T(8,128)(2,1)S(1)}, bf16[256,1024]{1,0:T(8,128)(2,1)S(1)}, u32[]{:S(2)}, u32[]{:S(2)}) collective-permute-start(bf16[256,1024]{1,0:T(8,128)(2,1)S(1)} %get-tuple-element.50), channel_id=1, source_target_pairs={{0,8},{8,16},{16,24},{1,9},{9,17},{17,25},{2,10},{10,18},{18,26},{... | collective-permute-start | bytes 1572872 | tf_op jit(solution)/shard_map/ppermute | solution.py:43
  338.6 12.7 %collective-permute-start.5 = (bf16[256,1024]{1,0:T(8,128)(2,1)S(1)}, bf16[256,1024]{1,0:T(8,128)(2,1)S(1)}, u32[]{:S(2)}, u32[]{:S(2)}) collective-permute-start(bf16[256,1024]{1,0:T(8,128)(2,1)S(1)} %fusion.541), channel_id=1, source_target_pairs={{0,8},{8,16},{16,24},{1,9},{9,17},{17,25},{2,10},{10,18},{18,26},{... | collective-permute-start | bytes 1572872 | tf_op jit(solution)/shard_map/ppermute | solution.py:43
  386.9 20.2 %collective-permute-start.7 = (bf16[256,1024]{1,0:T(8,128)(2,1)S(1)}, bf16[256,1024]{1,0:T(8,128)(2,1)S(1)}, u32[]{:S(2)}, u32[]{:S(2)}) collective-permute-start(bf16[256,1024]{1,0:T(8,128)(2,1)S(1)} %fusion.553), channel_id=1, source_target_pairs={{0,8},{8,16},{16,24},{1,9},{9,17},{17,25},{2,10},{10,18},{18,26},{... | collective-permute-start | bytes 1572872 | tf_op jit(solution)/shard_map/ppermute | solution.py:43
  402.8 10.5 %collective-permute-start.2 = (bf16[256,1024]{1,0:T(8,128)(2,1)S(1)}, bf16[256,1024]{1,0:T(8,128)(2,1)S(1)}, u32[]{:S(2)}, u32[]{:S(2)}) collective-permute-start(bf16[256,1024]{1,0:T(8,128)(2,1)S(1)} %get-tuple-element.62), channel_id=1, source_target_pairs={{0,8},{8,16},{16,24},{1,9},{9,17},{17,25},{2,10},{10,18},{18,26},{... | collective-permute-start | bytes 1572872 | tf_op jit(solution)/shard_map/ppermute | solution.py:43
  449.6 19.6 %collective-permute-start.4 = (bf16[256,1024]{1,0:T(8,128)(2,1)}, bf16[256,1024]{1,0:T(8,128)(2,1)S(1)}, u32[]{:S(2)}, u32[]{:S(2)}) collective-permute-start(bf16[256,1024]{1,0:T(8,128)(2,1)} %get-tuple-element.68), channel_id=1, source_target_pairs={{0,8},{8,16},{16,24},{1,9},{9,17},{17,25},{2,10},{10,18},{18,26},{... | collective-permute-start | bytes 1572872 | tf_op jit(solution)/shard_map/ppermute | solution.py:43
  464.7 32.2 %collective-permute-start.9 = (bf16[256,1024]{1,0:T(8,128)(2,1)S(1)}, bf16[256,1024]{1,0:T(8,128)(2,1)S(1)}, u32[]{:S(2)}, u32[]{:S(2)}) collective-permute-start(bf16[256,1024]{1,0:T(8,128)(2,1)S(1)} %fusion.565), channel_id=1, source_target_pairs={{0,8},{8,16},{16,24},{1,9},{9,17},{17,25},{2,10},{10,18},{18,26},{... | collective-permute-start | bytes 1572872 | tf_op jit(solution)/shard_map/ppermute | solution.py:43
  493.4 8.8 %collective-permute-start.6 = (bf16[256,1024]{1,0:T(8,128)(2,1)S(1)}, bf16[256,1024]{1,0:T(8,128)(2,1)S(1)}, u32[]{:S(2)}, u32[]{:S(2)}) collective-permute-start(bf16[256,1024]{1,0:T(8,128)(2,1)S(1)} %get-tuple-element.72), channel_id=1, source_target_pairs={{0,8},{8,16},{16,24},{1,9},{9,17},{17,25},{2,10},{10,18},{18,26},{... | collective-permute-start | bytes 1572872 | tf_op jit(solution)/shard_map/ppermute | solution.py:43
  537.4 18.7 %collective-permute-start.11 = (bf16[256,1024]{1,0:T(8,128)(2,1)S(1)}, bf16[256,1024]{1,0:T(8,128)(2,1)S(1)}, u32[]{:S(2)}, u32[]{:S(2)}) collective-permute-start(bf16[256,1024]{1,0:T(8,128)(2,1)S(1)} %fusion.577), channel_id=1, source_target_pairs={{0,8},{8,16},{16,24},{1,9},{9,17},{17,25},{2,10},{10,18},{18,26},{... | collective-permute-start | bytes 1572872 | tf_op jit(solution)/shard_map/ppermute | solution.py:43
  553.3 8.6 %collective-permute-start.8 = (bf16[256,1024]{1,0:T(8,128)(2,1)S(1)}, bf16[256,1024]{1,0:T(8,128)(2,1)S(1)}, u32[]{:S(2)}, u32[]{:S(2)}) collective-permute-start(bf16[256,1024]{1,0:T(8,128)(2,1)S(1)} %get-tuple-element.78), channel_id=1, source_target_pairs={{0,8},{8,16},{16,24},{1,9},{9,17},{17,25},{2,10},{10,18},{18,26},{... | collective-permute-start | bytes 1572872 | tf_op jit(solution)/shard_map/ppermute | solution.py:43
  597.6 11.1 %collective-permute-start.10 = (bf16[256,1024]{1,0:T(8,128)(2,1)S(1)}, bf16[256,1024]{1,0:T(8,128)(2,1)S(1)}, u32[]{:S(2)}, u32[]{:S(2)}) collective-permute-start(bf16[256,1024]{1,0:T(8,128)(2,1)S(1)} %get-tuple-element.84), channel_id=1, source_target_pairs={{0,8},{8,16},{16,24},{1,9},{9,17},{17,25},{2,10},{10,18},{18,26},{... | collective-permute-start | bytes 1572872 | tf_op jit(solution)/shard_map/ppermute | solution.py:43
Sparse Core Ops, SparseCore 0:
  9.8 58.2 all-gather.8
  70.0 53.8 all-gather.10
  125.8 55.4 all-gather.12
  183.1 53.8 all-gather.14

commit v2 on v0

v2 whole, which is shorter than its diff:
```python
import functools

import jax
import jax.numpy as jnp
from jax import lax
from jax.experimental import pallas as pl
from jax.experimental.pallas import tpu as pltpu
from jax.sharding import PartitionSpec as P

EPS = 1e-5
MESH = pl.DeviceIdType.MESH
ROWS = 32


def _kernel(x_hbm, g_ref, w1_hbm, w2_hbm, out_hbm, w1v, w2v, inbuf, hbuf, ybuf, acc, abuf,
            xsem, lsem, rsem, ssem, fsem, zrsem, zssem, osem, *, S):
    s = lax.axis_index('stage')
    tp = lax.axis_index('tp')
    c = tp % 2
    sib = tp + 1 - 2 * c
    nbr = (tp + 2 - 4 * ((tp // 2) % 2), tp + 4 - 8 * (tp // 4))
    NB, _, _, D, U = w1v.shape
    M, T, _ = inbuf.shape

    def slot(b, j, k):
        return w1v.at[b, j, k], w2v.at[b, j, pl.ds(pl.multiple_of(k * U, U), U)]

    def load(b, q):
        d1, d2 = slot(b, 0, 2 * c + q)
        return (pltpu.make_async_copy(w1_hbm.at[0, b, :, pl.ds(q * U, U)], d1, lsem.at[b, q, 0]),
                pltpu.make_async_copy(w2_hbm.at[0, b, pl.ds(q * U, U)], d2, lsem.at[b, q, 1]))

    def copies(src, dst, ssems, rsems, to):
        return tuple(pltpu.make_async_remote_copy(
            src_ref=src[w], dst_ref=dst[w], send_sem=ssems.at[w], recv_sem=rsems.at[w],
            device_id=(s, to), device_id_type=MESH) for w in range(2))

    def send(b, j, l):
        src = slot(b, 0, 2 * c + l) if j == 1 else (
            slot(b, 0, 2 * c + 1 - l) if j == 2 else slot(b, 1, 2 * c + 1 - l))
        return copies(src, slot(b, j, 2 * c + l), ssem.at[b, j - 1, l], rsem.at[b, j, 2 * c + l], nbr[l])

    def share(b, j, l):
        u = slot(b, j, 2 * c + l)
        return copies(u, u, fsem.at[b, j, l], rsem.at[b, j, 2 * c + l], sib)

    def arrived(b, j, k):
        u = slot(b, j, k)
        for cp in copies(u, u, fsem.at[b, j, 0], rsem.at[b, j, k], sib):
            cp.wait_recv()

    def start(cps):
        for cp in cps:
            cp.start()

    def zsend(m):
        return pltpu.make_async_remote_copy(
            src_ref=ybuf.at[m], dst_ref=inbuf.at[m], send_sem=zssem.at[m], recv_sem=zrsem.at[m],
            device_id=(s + 1, tp), device_id_type=MESH)

    def out(m):
        return pltpu.make_async_copy(ybuf.at[m], out_hbm.at[0, m], osem.at[m])

    xin = pltpu.make_async_copy(x_hbm, inbuf, xsem)

    @pl.when(s == 0)
    def _():
        xin.start()
    for b in range(NB):
        for q in range(2):
            start(load(b, q))

    barrier = pltpu.get_barrier_semaphore()
    for to in (sib, *nbr):
        pl.semaphore_signal(barrier, inc=1, device_id=(s, to), device_id_type=MESH)

    @pl.when(s > 0)
    def _():
        pl.semaphore_signal(barrier, inc=1, device_id=(s - 1, tp), device_id_type=MESH)

    @pl.when(s < S - 1)
    def _():
        pl.semaphore_signal(barrier, inc=1, device_id=(s + 1, tp), device_id_type=MESH)
    edge = (s == 0) | (s == S - 1)

    @pl.when(edge)
    def _():
        pl.semaphore_wait(barrier, 4)

    @pl.when(jnp.logical_not(edge))
    def _():
        pl.semaphore_wait(barrier, 5)

    def own(b):
        for q in range(2):
            for cp in load(b, q):
                cp.wait()
        for j in (1, 2):
            for l in range(2):
                start(send(b, j, l))
        for l in range(2):
            start(share(b, 0, l))

    def relay(b, j):
        for l in range(2):
            arrived(b, j, 2 * c + l)
        if j == 1:
            for l in range(2):
                start(send(b, 3, l))
        for l in range(2):
            start(share(b, j, l))
        if j == 1 and b + 1 < NB:
            own(b + 1)

    def others(b, j):
        for l in range(2):
            arrived(b, j, 2 * (1 - c) + l)

    def norm(m, b, y_ref):
        g = g_ref[0, pl.ds(b, 1), :].astype(jnp.float32)
        for r in range(0, T, ROWS):
            rows = pl.ds(r, ROWS)
            yf = y_ref[m, rows, :].astype(jnp.bfloat16).astype(jnp.float32)
            acc[m, rows, :] = yf
            yc = yf - jnp.mean(yf, axis=-1, keepdims=True)
            var = jnp.mean(jnp.square(yc), axis=-1, keepdims=True)
            hbuf[m, rows, :] = (yc * lax.rsqrt(var + EPS) * g).astype(jnp.bfloat16)

    def mlp(m, b, j):
        h = hbuf[m]
        for k in range(4):
            z = jnp.dot(h, w1v[b, j, k], preferred_element_type=jnp.float32)
            abuf[:, k * U:(k + 1) * U] = jax.nn.gelu(z).astype(jnp.bfloat16)
        acc[m] += jnp.dot(abuf[...], w2v[b, j], preferred_element_type=jnp.float32)

    def finish(m):
        ybuf[m] = acc[m].astype(jnp.bfloat16)
        out(m).start()

        @pl.when(s < S - 1)
        def _():
            zsend(m).start()

    def each(body):
        def step(m, carry):
            body(m)
            return carry
        lax.fori_loop(0, M, step, 0)

    own(0)

    @pl.when(s == 0)
    def _():
        xin.wait()
        each(lambda m: norm(m, 0, inbuf))
        for b in range(NB):
            for j in range(4):
                if j:
                    relay(b, j)
                others(b, j)

                def body(m, b=b, j=j):
                    mlp(m, b, j)
                    if j == 3 and b < NB - 1:
                        norm(m, b + 1, acc)
                    if j == 3 and b == NB - 1:
                        finish(m)
                each(body)

    @pl.when(s > 0)
    def _():
        for b in range(NB):
            for j in range(1, 4):
                relay(b, j)
        for b in range(NB):
            for j in range(4):
                others(b, j)

        def body(m):
            pltpu.make_async_remote_copy(
                src_ref=ybuf.at[m], dst_ref=inbuf.at[m], send_sem=zssem.at[m], recv_sem=zrsem.at[m],
                device_id=(s, tp), device_id_type=MESH).wait_recv()
            for b in range(NB):
                norm(m, b, inbuf if b == 0 else acc)

                def step(j, carry, b=b):
                    mlp(m, b, j)
                    return carry
                lax.fori_loop(0, 4, step, 0)
            finish(m)
        each(body)

    for b in range(NB):
        for l in range(2):
            for j in range(4):
                for cp in share(b, j, l):
                    cp.wait_send()
                if j:
                    for cp in send(b, j, l):
                        cp.wait_send()
    for m in range(M):
        out(m).wait()

    @pl.when(s < S - 1)
    def _():
        for m in range(M):
            zsend(m).wait_send()


def solution(mesh):
    S = mesh.shape['stage']

    def local(x, g, w1, w2):
        M, T, D = x.shape
        NB, F = w1.shape[1], w1.shape[3]
        U = F // 2
        bf, f32 = jnp.bfloat16, jnp.float32
        dma = pltpu.SemaphoreType.DMA
        return pl.pallas_call(
            functools.partial(_kernel, S=S),
            out_shape=jax.ShapeDtypeStruct((1, M, T, D), bf),
            in_specs=[pl.BlockSpec(memory_space=pl.ANY), pl.BlockSpec(memory_space=pltpu.VMEM),
                      pl.BlockSpec(memory_space=pl.ANY), pl.BlockSpec(memory_space=pl.ANY)],
            out_specs=pl.BlockSpec(memory_space=pl.ANY),
            scratch_shapes=[
                pltpu.VMEM((NB, 4, 4, D, U), bf), pltpu.VMEM((NB, 4, 4 * U, D), bf),
                pltpu.VMEM((M, T, D), bf), pltpu.VMEM((M, T, D), bf), pltpu.VMEM((M, T, D), bf),
                pltpu.VMEM((M, T, D), f32), pltpu.VMEM((T, 4 * U), bf),
                dma(()), dma((NB, 2, 2)), dma((NB, 4, 4, 2)), dma((NB, 3, 2, 2)), dma((NB, 4, 2, 2)),
                dma((M,)), dma((M,)), dma((M,)),
            ],
            compiler_params=pltpu.CompilerParams(
                collective_id=0, has_side_effects=True, vmem_limit_bytes=67043328),
        )(x, g, w1, w2)

    return jax.shard_map(
        local, mesh=mesh,
        in_specs=(P(None, 'tp', None), P('stage', None, None),
                  P('stage', None, None, 'tp'), P('stage', None, 'tp', None)),
        out_specs=P('stage', None, 'tp', None), check_vma=False)
```

time: 2400 us -> 308 us (0.13)
  waiting for transfers between devices: 2050 us -> 0 us
  Pallas kernels: 0 us -> 303 us
  matrix products: 214 us -> 0 us
  other arithmetic: 84.7 us -> 0 us
    reduce_scatter x22 -> x0, waiting for transfers between devices: 1100 us -> none  [_block(): r = lax.psum_scatter(p, 'tp', scatter_dimension=0, tiled=True)]
    all_gather x22 -> x0, waiting for transfers between devices: 800 us -> none  [_block(): h = lax.all_gather(_ln(y, g), 'tp', axis=0, tiled=True)]
    pallas_call x0 -> x1, Pallas kernels: none -> 303 us  [local(): pl.pallas_call(functools.partial(_kernel, S=S), out_shape=jax.ShapeDtypeS...]
    dot_general x22 -> x0, matrix products: 214 us -> none  [_block(): p = jnp.dot(a, w2, preferred_element_type=jnp.float32).astype(jnp.bfloat16)]
    ppermute x10 -> x0, waiting for transfers between devices: 140 us -> none  [local(): recv = lax.ppermute(y, 'stage', fwd)]
    reduce_sum x44 -> x0, other arithmetic: 35.5 us -> none  [the longest x22 28.3 us: _ln(): mu = jnp.mean(yf, axis=-1, keepdims=True)]
    convert_element_type x23 -> x0, other arithmetic: 26 us -> none  [the longest x22 25.2 us: _ln(): ((yf - mu) * lax.rsqrt(var + EPS) * g.astype(jnp.float32)).astype(jnp.bfl...]
  transfers between devices with their start and end apart: 54 -> 0, of which waited for: 54 -> 0; matrix products, arithmetic and copies ran while one was open for 1% -> 0% of each run, Pallas kernels for 0% -> 0%
where the time goes in v2:
time: 308 us
  Pallas kernels  303 us (98%)
  local copies, waits for them, and re-layouts  4.64 us (2%)
    pallas_call x1, Pallas kernels, local(): pl.pallas_call(functools.partial(_kernel, S=S), out_shape=jax.ShapeDtypeS...  303 us

profile of v2, /device:TPU:24, one launch (start us, length us, event | category | flops | bytes accessed | tf_op | source)
XLA Modules:
  0.0 308.0 jit_solution(2836868713540526841)
XLA Ops:
  0.0 303.4 %shard_map.46 = bf16[1,8,256,1024]{3,2,1,0:T(8,128)(2,1)} custom-call(bf16[8,256,1024]{2,1,0:T(8,128)(2,1)} %x_hbm.1, bf16[1,2,1024]{2,1,0:T(2,128)(2,1)} %g_ref.1, bf16[1,2,1024,512]{3,2,1,0:T(8,128)(2,1)} %w1_hbm.1, bf16[1,2,512,1024]{3,2,1,0:T(8,128)(2,1)} %w2_hbm.1), custom_call_target="tpu_custom_call" | custom-call | tf_op jit(solution)/shard_map/pallas_call | solution.py:219
  303.4 4.6 %copy.6 = bf16[1,8,256,1024]{3,2,1,0:T(8,128)(2,1)} copy(bf16[1,8,256,1024]{3,2,1,0:T(8,128)(2,1)} %shard_map.46) | data formatting | bytes 8388608

commit v3 on v2

--- a/solution.py
+++ b/solution.py
@@ -10,6 +10,7 @@
 EPS = 1e-5
 MESH = pl.DeviceIdType.MESH
 ROWS = 32
+SPLIT = 2
 
 
 def _kernel(x_hbm, g_ref, w1_hbm, w2_hbm, out_hbm, w1v, w2v, inbuf, hbuf, ybuf, acc, abuf,
@@ -126,12 +127,15 @@
             var = jnp.mean(jnp.square(yc), axis=-1, keepdims=True)
             hbuf[m, rows, :] = (yc * lax.rsqrt(var + EPS) * g).astype(jnp.bfloat16)
 
-    def mlp(m, b, j):
+    def mlp(m, b, steps):
         h = hbuf[m]
-        for k in range(4):
-            z = jnp.dot(h, w1v[b, j, k], preferred_element_type=jnp.float32)
-            abuf[:, k * U:(k + 1) * U] = jax.nn.gelu(z).astype(jnp.bfloat16)
-        acc[m] += jnp.dot(abuf[...], w2v[b, j], preferred_element_type=jnp.float32)
+        n = len(steps) * 4 * U
+        for i, j in enumerate(steps):
+            for k in range(4):
+                z = jnp.dot(h, w1v[b, j, k], preferred_element_type=jnp.float32)
+                abuf[:, (4 * i + k) * U:(4 * i + k + 1) * U] = jax.nn.gelu(z).astype(jnp.bfloat16)
+        w2 = w2v[b, steps[0]:steps[0] + len(steps)].reshape(n, D)
+        acc[m] += jnp.dot(abuf[:, :n], w2, preferred_element_type=jnp.float32)
 
     def finish(m):
         ybuf[m] = acc[m].astype(jnp.bfloat16)
@@ -160,7 +164,7 @@
                 others(b, j)
 
                 def body(m, b=b, j=j):
-                    mlp(m, b, j)
+                    mlp(m, b, (j,))
                     if j == 3 and b < NB - 1:
                         norm(m, b + 1, acc)
                     if j == 3 and b == NB - 1:
@@ -182,11 +186,7 @@
                 device_id=(s, tp), device_id_type=MESH).wait_recv()
             for b in range(NB):
                 norm(m, b, inbuf if b == 0 else acc)
-
-                def step(j, carry, b=b):
-                    mlp(m, b, j)
-                    return carry
-                lax.fori_loop(0, 4, step, 0)
+                mlp(m, b, (0, 1, 2, 3))
             finish(m)
         each(body)
 
@@ -212,11 +212,13 @@
 
     def local(x, g, w1, w2):
         M, T, D = x.shape
+        M, T = M * SPLIT, T // SPLIT
+        x = x.reshape(M, T, D)
         NB, F = w1.shape[1], w1.shape[3]
         U = F // 2
         bf, f32 = jnp.bfloat16, jnp.float32
         dma = pltpu.SemaphoreType.DMA
-        return pl.pallas_call(
+        y = pl.pallas_call(
             functools.partial(_kernel, S=S),
             out_shape=jax.ShapeDtypeStruct((1, M, T, D), bf),
             in_specs=[pl.BlockSpec(memory_space=pl.ANY), pl.BlockSpec(memory_space=pltpu.VMEM),
@@ -225,13 +227,14 @@
             scratch_shapes=[
                 pltpu.VMEM((NB, 4, 4, D, U), bf), pltpu.VMEM((NB, 4, 4 * U, D), bf),
                 pltpu.VMEM((M, T, D), bf), pltpu.VMEM((M, T, D), bf), pltpu.VMEM((M, T, D), bf),
-                pltpu.VMEM((M, T, D), f32), pltpu.VMEM((T, 4 * U), bf),
+                pltpu.VMEM((M, T, D), f32), pltpu.VMEM((T, 16 * U), bf),
                 dma(()), dma((NB, 2, 2)), dma((NB, 4, 4, 2)), dma((NB, 3, 2, 2)), dma((NB, 4, 2, 2)),
                 dma((M,)), dma((M,)), dma((M,)),
             ],
             compiler_params=pltpu.CompilerParams(
                 collective_id=0, has_side_effects=True, vmem_limit_bytes=67043328),
         )(x, g, w1, w2)
+        return y.reshape(1, M // SPLIT, T * SPLIT, D)
 
     return jax.shard_map(
         local, mesh=mesh,

time: 308 us -> 276 us (0.90)
  Pallas kernels: 303 us -> 272 us
    pallas_call x1, Pallas kernels: 303 us -> 272 us  [local(): pl.pallas_call(functools.partial(_kernel, S=S), out_shape=jax.ShapeDtypeS...]
where the time goes in v3:
time: 276 us
  Pallas kernels  272 us (99%)
  local copies, waits for them, and re-layouts  4.64 us (2%)
    pallas_call x1, Pallas kernels, local(): pl.pallas_call(functools.partial(_kernel, S=S), out_shape=jax.ShapeDtypeS...  272 us

profile of v3, /device:TPU:24, one launch (start us, length us, event | category | flops | bytes accessed | tf_op | source)
XLA Modules:
  0.0 276.2 jit_solution(4001527177016790118)
XLA Ops:
  0.0 271.5 %shard_map.46 = bf16[1,16,128,1024]{3,2,1,0:T(8,128)(2,1)} custom-call(bf16[16,128,1024]{2,1,0:T(8,128)(2,1)} %bitcast.3, bf16[1,2,1024]{2,1,0:T(2,128)(2,1)} %g_ref.1, bf16[1,2,1024,512]{3,2,1,0:T(8,128)(2,1)} %w1_hbm.1, bf16[1,2,512,1024]{3,2,1,0:T(8,128)(2,1)} %w2_hbm.1), custom_call_target="tpu_custom_call" | custom-call | tf_op jit(solution)/shard_map/pallas_call | solution.py:221
  271.5 4.6 %copy.6 = bf16[1,8,256,1024]{3,2,1,0:T(8,128)(2,1)} copy(bf16[1,8,256,1024]{3,2,1,0:T(8,128)(2,1)} %bitcast.2) | data formatting | bytes 8388608

commit v4 on v3

--- a/solution.py
+++ b/solution.py
@@ -13,8 +13,8 @@
 SPLIT = 2
 
 
-def _kernel(x_hbm, g_ref, w1_hbm, w2_hbm, out_hbm, w1v, w2v, inbuf, hbuf, ybuf, acc, abuf,
-            xsem, lsem, rsem, ssem, fsem, zrsem, zssem, osem, *, S):
+def _kernel(x_hbm, g_ref, w1_hbm, w2_hbm, out_hbm, w1v, w2v, inbuf, hbuf, ybuf, acc, abuf, up1, up2, over1, over2,
+            xsem, lsem, rsem, ssem, fsem, usem, osem2, oss, dss, zrsem, zssem, osem, *, S):
     s = lax.axis_index('stage')
     tp = lax.axis_index('tp')
     c = tp % 2
@@ -22,54 +22,65 @@
     nbr = (tp + 2 - 4 * ((tp // 2) % 2), tp + 4 - 8 * (tp // 4))
     NB, _, _, D, U = w1v.shape
     M, T, _ = inbuf.shape
-
-    def slot(b, j, k):
-        return w1v.at[b, j, k], w2v.at[b, j, pl.ds(pl.multiple_of(k * U, U), U)]
-
-    def load(b, q):
-        d1, d2 = slot(b, 0, 2 * c + q)
-        return (pltpu.make_async_copy(w1_hbm.at[0, b, :, pl.ds(q * U, U)], d1, lsem.at[b, q, 0]),
-                pltpu.make_async_copy(w2_hbm.at[0, b, pl.ds(q * U, U)], d2, lsem.at[b, q, 1]))
-
-    def copies(src, dst, ssems, rsems, to):
-        return tuple(pltpu.make_async_remote_copy(
-            src_ref=src[w], dst_ref=dst[w], send_sem=ssems.at[w], recv_sem=rsems.at[w],
-            device_id=(s, to), device_id_type=MESH) for w in range(2))
-
-    def send(b, j, l):
-        src = slot(b, 0, 2 * c + l) if j == 1 else (
-            slot(b, 0, 2 * c + 1 - l) if j == 2 else slot(b, 1, 2 * c + 1 - l))
-        return copies(src, slot(b, j, 2 * c + l), ssem.at[b, j - 1, l], rsem.at[b, j, 2 * c + l], nbr[l])
-
-    def share(b, j, l):
-        u = slot(b, j, 2 * c + l)
-        return copies(u, u, fsem.at[b, j, l], rsem.at[b, j, 2 * c + l], sib)
-
-    def arrived(b, j, k):
-        u = slot(b, j, k)
-        for cp in copies(u, u, fsem.at[b, j, 0], rsem.at[b, j, k], sib):
-            cp.wait_recv()
-
-    def start(cps):
-        for cp in cps:
-            cp.start()
+    LW = [(l, w) for w in range(2) for l in range(2)]
+
+    def slot(b, j, k, w):
+        if w == 0:
+            return w1v.at[b, j, k]
+        return w2v.at[b, j, pl.ds(pl.multiple_of(k * U, U), U)]
+
+    def load(b, q, w):
+        src = w1_hbm.at[0, b, :, pl.ds(q * U, U)] if w == 0 else w2_hbm.at[0, b, pl.ds(q * U, U)]
+        return pltpu.make_async_copy(src, slot(b, 0, 2 * c + q, w), lsem.at[b, q, w])
+
+    def remote(src, dst, ssem_, rsem_, stage, to):
+        return pltpu.make_async_remote_copy(src_ref=src, dst_ref=dst, send_sem=ssem_, recv_sem=rsem_,
+                                            device_id=(stage, to), device_id_type=MESH)
+
+    def send(b, j, l, w):
+        src = (slot(b, 0, 2 * c + l, w), slot(b, 0, 2 * c + 1 - l, w), slot(b, 1, 2 * c + 1 - l, w))[j - 1]
+        return remote(src, slot(b, j, 2 * c + l, w), ssem.at[b, j - 1, l, w], rsem.at[b, j, 2 * c + l, w], s, nbr[l])
+
+    def share(b, j, l, w):
+        u = slot(b, j, 2 * c + l, w)
+        return remote(u, u, fsem.at[b, j, l, w], rsem.at[b, j, 2 * c + l, w], s, sib)
+
+    def arrived(b, j, k, w):
+        u = slot(b, j, k, w)
+        remote(u, u, fsem.at[b, j, 0, w], rsem.at[b, j, k, w], s, sib).wait_recv()
+
+    def helped(w):
+        return (s >= w) & (s < S - 1)
+
+    def helper(w):
+        return s >= w + 1
+
+    up, over = (up1, up2), (over1, over2)
+
+    def go_up(l, w):
+        return remote(slot(1, 0, 2 * c + 1 - l, w), up[w].at[l], ssem.at[1, 1, l, w], usem.at[l, w], s + 1, tp)
+
+    def go_over(l, w):
+        return remote(up[w].at[l], over[w].at[l], oss.at[l, w], osem2.at[l, w], s, nbr[l])
+
+    def go_down(l, w):
+        return remote(over[w].at[l], slot(1, 2, 2 * c + l, w), dss.at[l, w], rsem.at[1, 2, 2 * c + l, w], s - 1, tp)
 
     def zsend(m):
-        return pltpu.make_async_remote_copy(
-            src_ref=ybuf.at[m], dst_ref=inbuf.at[m], send_sem=zssem.at[m], recv_sem=zrsem.at[m],
-            device_id=(s + 1, tp), device_id_type=MESH)
+        return remote(ybuf.at[m], inbuf.at[m], zssem.at[m], zrsem.at[m], s + 1, tp)
 
     def out(m):
         return pltpu.make_async_copy(ybuf.at[m], out_hbm.at[0, m], osem.at[m])
 
     xin = pltpu.make_async_copy(x_hbm, inbuf, xsem)
-
-    @pl.when(s == 0)
-    def _():
-        xin.start()
     for b in range(NB):
         for q in range(2):
-            start(load(b, q))
+            for w in range(2):
+                load(b, q, w).start()
+
+    @pl.when(s == 0)
+    def _():
+        xin.start()
 
     barrier = pltpu.get_barrier_semaphore()
     for to in (sib, *nbr):
@@ -92,30 +103,41 @@
     def _():
         pl.semaphore_wait(barrier, 5)
 
-    def own(b):
-        for q in range(2):
-            for cp in load(b, q):
-                cp.wait()
-        for j in (1, 2):
+    for l, w in LW:
+        load(0, l, w).wait()
+    for j in (1, 2):
+        for l, w in LW:
+            send(0, j, l, w).start()
+    for l, w in LW:
+        load(1, l, w).wait()
+    for w in range(2):
+        @pl.when(helped(w))
+        def _(w=w):
             for l in range(2):
-                start(send(b, j, l))
-        for l in range(2):
-            start(share(b, 0, l))
-
-    def relay(b, j):
-        for l in range(2):
-            arrived(b, j, 2 * c + l)
-        if j == 1:
-            for l in range(2):
-                start(send(b, 3, l))
-        for l in range(2):
-            start(share(b, j, l))
-        if j == 1 and b + 1 < NB:
-            own(b + 1)
+                go_up(l, w).start()
+    for b in range(NB):
+        for l, w in LW:
+            share(b, 0, l, w).start()
+
+    def own_next():
+        for l, w in LW:
+            send(1, 1, l, w).start()
+        for w in range(2):
+            @pl.when(jnp.logical_not(helped(w)))
+            def _(w=w):
+                for l in range(2):
+                    send(1, 2, l, w).start()
+
+    def relay(b, j, on):
+        for l, w in LW:
+            arrived(b, j, 2 * c + l, w)
+            if on:
+                send(b, 3, 1 - l, w).start()
+            share(b, j, l, w).start()
 
     def others(b, j):
-        for l in range(2):
-            arrived(b, j, 2 * (1 - c) + l)
+        for l, w in LW:
+            arrived(b, j, 2 * (1 - c) + l, w)
 
     def norm(m, b, y_ref):
         g = g_ref[0, pl.ds(b, 1), :].astype(jnp.float32)
@@ -151,8 +173,6 @@
             return carry
         lax.fori_loop(0, M, step, 0)
 
-    own(0)
-
     @pl.when(s == 0)
     def _():
         xin.wait()
@@ -160,7 +180,9 @@
         for b in range(NB):
             for j in range(4):
                 if j:
-                    relay(b, j)
+                    relay(b, j, j == 1)
+                if (b, j) == (0, 1):
+                    own_next()
                 others(b, j)
 
                 def body(m, b=b, j=j):
@@ -173,17 +195,33 @@
 
     @pl.when(s > 0)
     def _():
-        for b in range(NB):
-            for j in range(1, 4):
-                relay(b, j)
+        relay(0, 1, False)
+        for w in range(2):
+            @pl.when(helper(w))
+            def _(w=w):
+                for l in range(2):
+                    go_up(l, w).wait_recv()
+                    go_over(l, w).start()
+        for l, w in LW:
+            send(0, 3, l, w).start()
+        own_next()
+        relay(0, 2, False)
+        for w in range(2):
+            @pl.when(helper(w))
+            def _(w=w):
+                for l in range(2):
+                    go_over(l, w).wait_recv()
+                    go_down(l, w).start()
+        relay(0, 3, False)
+        relay(1, 1, True)
+        relay(1, 2, False)
+        relay(1, 3, False)
         for b in range(NB):
             for j in range(4):
                 others(b, j)
 
         def body(m):
-            pltpu.make_async_remote_copy(
-                src_ref=ybuf.at[m], dst_ref=inbuf.at[m], send_sem=zssem.at[m], recv_sem=zrsem.at[m],
-                device_id=(s, tp), device_id_type=MESH).wait_recv()
+            zsend(m).wait_recv()
             for b in range(NB):
                 norm(m, b, inbuf if b == 0 else acc)
                 mlp(m, b, (0, 1, 2, 3))
@@ -191,13 +229,17 @@
         each(body)
 
     for b in range(NB):
-        for l in range(2):
-            for j in range(4):
-                for cp in share(b, j, l):
-                    cp.wait_send()
+        for j in range(4):
+            for l, w in LW:
+                share(b, j, l, w).wait_send()
                 if j:
-                    for cp in send(b, j, l):
-                        cp.wait_send()
+                    send(b, j, l, w).wait_send()
+    for w in range(2):
+        @pl.when(helper(w))
+        def _(w=w):
+            for l in range(2):
+                go_over(l, w).wait_send()
+                go_down(l, w).wait_send()
     for m in range(M):
         out(m).wait()
 
@@ -228,7 +270,9 @@
                 pltpu.VMEM((NB, 4, 4, D, U), bf), pltpu.VMEM((NB, 4, 4 * U, D), bf),
                 pltpu.VMEM((M, T, D), bf), pltpu.VMEM((M, T, D), bf), pltpu.VMEM((M, T, D), bf),
                 pltpu.VMEM((M, T, D), f32), pltpu.VMEM((T, 16 * U), bf),
+                pltpu.VMEM((2, D, U), bf), pltpu.VMEM((2, U, D), bf), pltpu.VMEM((2, D, U), bf), pltpu.VMEM((2, U, D), bf),
                 dma(()), dma((NB, 2, 2)), dma((NB, 4, 4, 2)), dma((NB, 3, 2, 2)), dma((NB, 4, 2, 2)),
+                dma((2, 2)), dma((2, 2)), dma((2, 2)), dma((2, 2)),
                 dma((M,)), dma((M,)), dma((M,)),
             ],
             compiler_params=pltpu.CompilerParams(

time: 276 us -> 275 us (level)
  no operation moved by 1% of the time
where the time goes in v4:
time: 275 us
  Pallas kernels  270 us (98%)
  local copies, waits for them, and re-layouts  4.64 us (2%)
    pallas_call x1, Pallas kernels, local(): pl.pallas_call(functools.partial(_kernel, S=S), out_shape=jax.ShapeDtypeS...  270 us

profile of v4, /device:TPU:24, one launch (start us, length us, event | category | flops | bytes accessed | tf_op | source)
XLA Modules:
  0.0 274.6 jit_solution(4612247741276042498)
XLA Ops:
  0.0 269.9 %shard_map.46 = bf16[1,16,128,1024]{3,2,1,0:T(8,128)(2,1)} custom-call(bf16[16,128,1024]{2,1,0:T(8,128)(2,1)} %bitcast.3, bf16[1,2,1024]{2,1,0:T(2,128)(2,1)} %g_ref.1, bf16[1,2,1024,512]{3,2,1,0:T(8,128)(2,1)} %w1_hbm.1, bf16[1,2,512,1024]{3,2,1,0:T(8,128)(2,1)} %w2_hbm.1), custom_call_target="tpu_custom_call" | custom-call | tf_op jit(solution)/shard_map/pallas_call | solution.py:263
  269.9 4.6 %copy.6 = bf16[1,8,256,1024]{3,2,1,0:T(8,128)(2,1)} copy(bf16[1,8,256,1024]{3,2,1,0:T(8,128)(2,1)} %bitcast.2) | data formatting | bytes 8388608

commit v5 on v4

--- a/solution.py
+++ b/solution.py
@@ -10,7 +10,8 @@
 EPS = 1e-5
 MESH = pl.DeviceIdType.MESH
 ROWS = 32
-SPLIT = 2
+WIDE = 256
+CHUNK, EDGE = 128, 64
 
 
 def _kernel(x_hbm, g_ref, w1_hbm, w2_hbm, out_hbm, w1v, w2v, inbuf, hbuf, ybuf, acc, abuf, up1, up2, over1, over2,
@@ -21,7 +22,7 @@
     sib = tp + 1 - 2 * c
     nbr = (tp + 2 - 4 * ((tp // 2) % 2), tp + 4 - 8 * (tp // 4))
     NB, _, _, D, U = w1v.shape
-    M, T, _ = inbuf.shape
+    R = inbuf.shape[0]
     LW = [(l, w) for w in range(2) for l in range(2)]
 
     def slot(b, j, k, w):
@@ -66,11 +67,28 @@
     def go_down(l, w):
         return remote(over[w].at[l], slot(1, 2, 2 * c + l, w), dss.at[l, w], rsem.at[1, 2, 2 * c + l, w], s - 1, tp)
 
-    def zsend(m):
-        return remote(ybuf.at[m], inbuf.at[m], zssem.at[m], zrsem.at[m], s + 1, tp)
-
-    def out(m):
-        return pltpu.make_async_copy(ybuf.at[m], out_hbm.at[0, m], osem.at[m])
+    mid = (R - 2 * EDGE) // CHUNK
+
+    def rows_of(i, n):
+        start = (0 if i == 0 else R - EDGE) if n == EDGE else EDGE + CHUNK * (i - 1)
+        return pl.ds(start if isinstance(start, int) else pl.multiple_of(start, EDGE), n)
+
+    def zsend(i, n):
+        r = rows_of(i, n)
+        return remote(ybuf.at[r], inbuf.at[r], zssem.at[i], zrsem.at[i], s + 1, tp)
+
+    def out(i, n):
+        r = rows_of(i, n)
+        return pltpu.make_async_copy(ybuf.at[r], out_hbm.at[r], osem.at[i])
+
+    def each(body):
+        body(0, EDGE)
+
+        def step(i, carry):
+            body(i, CHUNK)
+            return carry
+        lax.fori_loop(1, mid + 1, step, 0)
+        body(mid + 1, EDGE)
 
     xin = pltpu.make_async_copy(x_hbm, inbuf, xsem)
     for b in range(NB):
@@ -139,59 +157,63 @@
         for l, w in LW:
             arrived(b, j, 2 * (1 - c) + l, w)
 
-    def norm(m, b, y_ref):
+    def norm(r0, n, b, y_ref):
         g = g_ref[0, pl.ds(b, 1), :].astype(jnp.float32)
-        for r in range(0, T, ROWS):
-            rows = pl.ds(r, ROWS)
-            yf = y_ref[m, rows, :].astype(jnp.bfloat16).astype(jnp.float32)
-            acc[m, rows, :] = yf
+        for r in range(0, n, ROWS):
+            rows = pl.ds(r0 + r, ROWS)
+            yf = y_ref[rows, :].astype(jnp.bfloat16).astype(jnp.float32)
+            acc[rows, :] = yf
             yc = yf - jnp.mean(yf, axis=-1, keepdims=True)
             var = jnp.mean(jnp.square(yc), axis=-1, keepdims=True)
-            hbuf[m, rows, :] = (yc * lax.rsqrt(var + EPS) * g).astype(jnp.bfloat16)
-
-    def mlp(m, b, steps):
-        h = hbuf[m]
+            hbuf[rows, :] = (yc * lax.rsqrt(var + EPS) * g).astype(jnp.bfloat16)
+
+    def mlp(rows, b, steps):
+        h = hbuf[rows, :]
         n = len(steps) * 4 * U
         for i, j in enumerate(steps):
             for k in range(4):
                 z = jnp.dot(h, w1v[b, j, k], preferred_element_type=jnp.float32)
-                abuf[:, (4 * i + k) * U:(4 * i + k + 1) * U] = jax.nn.gelu(z).astype(jnp.bfloat16)
+                abuf[:rows.size, (4 * i + k) * U:(4 * i + k + 1) * U] = jax.nn.gelu(z).astype(jnp.bfloat16)
         w2 = w2v[b, steps[0]:steps[0] + len(steps)].reshape(n, D)
-        acc[m] += jnp.dot(abuf[:, :n], w2, preferred_element_type=jnp.float32)
-
-    def finish(m):
-        ybuf[m] = acc[m].astype(jnp.bfloat16)
-        out(m).start()
+        acc[rows, :] += jnp.dot(abuf[:rows.size, :n], w2, preferred_element_type=jnp.float32)
+
+    def finish(i, n):
+        rows = rows_of(i, n)
+        ybuf[rows, :] = acc[rows, :].astype(jnp.bfloat16)
 
         @pl.when(s < S - 1)
         def _():
-            zsend(m).start()
-
-    def each(body):
-        def step(m, carry):
-            body(m)
-            return carry
-        lax.fori_loop(0, M, step, 0)
+            zsend(i, n).start()
+        out(i, n).start()
 
     @pl.when(s == 0)
     def _():
+        def wide(body):
+            def step(i, carry):
+                body(pl.multiple_of(i * WIDE, WIDE))
+                return carry
+            lax.fori_loop(0, R // WIDE, step, 0)
+
         xin.wait()
-        each(lambda m: norm(m, 0, inbuf))
+        wide(lambda r0: norm(r0, WIDE, 0, inbuf))
         for b in range(NB):
             for j in range(4):
                 if j:
                     relay(b, j, j == 1)
-                if (b, j) == (0, 1):
+                if (b, j) == (0, 2):
                     own_next()
                 others(b, j)
-
-                def body(m, b=b, j=j):
-                    mlp(m, b, (j,))
-                    if j == 3 and b < NB - 1:
-                        norm(m, b + 1, acc)
-                    if j == 3 and b == NB - 1:
-                        finish(m)
-                each(body)
+                if (b, j) == (NB - 1, 3):
+                    def last(i, n):
+                        mlp(rows_of(i, n), NB - 1, (3,))
+                        finish(i, n)
+                    each(last)
+                else:
+                    def body(r0, b=b, j=j):
+                        mlp(pl.ds(r0, WIDE), b, (j,))
+                        if j == 3:
+                            norm(r0, WIDE, b + 1, acc)
+                    wide(body)
 
     @pl.when(s > 0)
     def _():
@@ -204,7 +226,6 @@
                     go_over(l, w).start()
         for l, w in LW:
             send(0, 3, l, w).start()
-        own_next()
         relay(0, 2, False)
         for w in range(2):
             @pl.when(helper(w))
@@ -212,6 +233,8 @@
                 for l in range(2):
                     go_over(l, w).wait_recv()
                     go_down(l, w).start()
+            if w == 0:
+                own_next()
         relay(0, 3, False)
         relay(1, 1, True)
         relay(1, 2, False)
@@ -220,12 +243,13 @@
             for j in range(4):
                 others(b, j)
 
-        def body(m):
-            zsend(m).wait_recv()
+        def body(i, n):
+            zsend(i, n).wait_recv()
+            rows = rows_of(i, n)
             for b in range(NB):
-                norm(m, b, inbuf if b == 0 else acc)
-                mlp(m, b, (0, 1, 2, 3))
-            finish(m)
+                norm(rows.start, n, b, inbuf if b == 0 else acc)
+                mlp(rows, b, (0, 1, 2, 3))
+            finish(i, n)
         each(body)
 
     for b in range(NB):
@@ -240,13 +264,14 @@
             for l in range(2):
                 go_over(l, w).wait_send()
                 go_down(l, w).wait_send()
-    for m in range(M):
-        out(m).wait()
-
-    @pl.when(s < S - 1)
-    def _():
-        for m in range(M):
-            zsend(m).wait_send()
+
+    def ended(i, n):
+        out(i, n).wait()
+
+        @pl.when(s < S - 1)
+        def _():
+            zsend(i, n).wait_send()
+    each(ended)
 
 
 def solution(mesh):
@@ -254,31 +279,31 @@
 
     def local(x, g, w1, w2):
         M, T, D = x.shape
-        M, T = M * SPLIT, T // SPLIT
-        x = x.reshape(M, T, D)
+        R = M * T
+        n = (R - 2 * EDGE) // CHUNK + 2
         NB, F = w1.shape[1], w1.shape[3]
         U = F // 2
         bf, f32 = jnp.bfloat16, jnp.float32
         dma = pltpu.SemaphoreType.DMA
         y = pl.pallas_call(
             functools.partial(_kernel, S=S),
-            out_shape=jax.ShapeDtypeStruct((1, M, T, D), bf),
+            out_shape=jax.ShapeDtypeStruct((R, D), bf),
             in_specs=[pl.BlockSpec(memory_space=pl.ANY), pl.BlockSpec(memory_space=pltpu.VMEM),
                       pl.BlockSpec(memory_space=pl.ANY), pl.BlockSpec(memory_space=pl.ANY)],
             out_specs=pl.BlockSpec(memory_space=pl.ANY),
             scratch_shapes=[
                 pltpu.VMEM((NB, 4, 4, D, U), bf), pltpu.VMEM((NB, 4, 4 * U, D), bf),
-                pltpu.VMEM((M, T, D), bf), pltpu.VMEM((M, T, D), bf), pltpu.VMEM((M, T, D), bf),
-                pltpu.VMEM((M, T, D), f32), pltpu.VMEM((T, 16 * U), bf),
+                pltpu.VMEM((R, D), bf), pltpu.VMEM((R, D), bf), pltpu.VMEM((R, D), bf),
+                pltpu.VMEM((R, D), f32), pltpu.VMEM((WIDE, 16 * U), bf),
                 pltpu.VMEM((2, D, U), bf), pltpu.VMEM((2, U, D), bf), pltpu.VMEM((2, D, U), bf), pltpu.VMEM((2, U, D), bf),
                 dma(()), dma((NB, 2, 2)), dma((NB, 4, 4, 2)), dma((NB, 3, 2, 2)), dma((NB, 4, 2, 2)),
                 dma((2, 2)), dma((2, 2)), dma((2, 2)), dma((2, 2)),
-                dma((M,)), dma((M,)), dma((M,)),
+                dma((n,)), dma((n,)), dma((n,)),
             ],
             compiler_params=pltpu.CompilerParams(
                 collective_id=0, has_side_effects=True, vmem_limit_bytes=67043328),
-        )(x, g, w1, w2)
-        return y.reshape(1, M // SPLIT, T * SPLIT, D)
+        )(x.reshape(R, D), g, w1, w2)
+        return y.reshape(1, M, T, D)
 
     return jax.shard_map(
         local, mesh=mesh,

time: 275 us -> 270 us (0.982)
  Pallas kernels: 270 us -> 265 us
    pallas_call x1, Pallas kernels: 270 us -> 265 us  [local(): pl.pallas_call(functools.partial(_kernel, S=S), out_shape=jax.ShapeDtypeS...]
where the time goes in v5:
time: 270 us
  Pallas kernels  265 us (98%)
  local copies, waits for them, and re-layouts  4.64 us (2%)
    pallas_call x1, Pallas kernels, local(): pl.pallas_call(functools.partial(_kernel, S=S), out_shape=jax.ShapeDtypeS...  265 us

profile of v5, /device:TPU:24, one launch (start us, length us, event | category | flops | bytes accessed | tf_op | source)
XLA Modules:
  0.0 269.5 jit_solution(13524247833084206947)
XLA Ops:
  0.0 264.9 %shard_map.46 = bf16[2048,1024]{1,0:T(8,128)(2,1)} custom-call(bf16[2048,1024]{1,0:T(8,128)(2,1)} %bitcast.3, bf16[1,2,1024]{2,1,0:T(2,128)(2,1)} %g_ref.1, bf16[1,2,1024,512]{3,2,1,0:T(8,128)(2,1)} %w1_hbm.1, bf16[1,2,512,1024]{3,2,1,0:T(8,128)(2,1)} %w2_hbm.1), custom_call_target="tpu_custom_call" | custom-call | tf_op jit(solution)/shard_map/pallas_call | solution.py:288
  264.9 4.6 %copy.6 = bf16[1,8,256,1024]{3,2,1,0:T(8,128)(2,1)} copy(bf16[1,8,256,1024]{3,2,1,0:T(8,128)(2,1)} %bitcast.2) | data formatting | bytes 8388608

commit v6 on v5

v6 whole, which is shorter than its diff:
```python
import functools

import jax
import jax.numpy as jnp
from jax import lax
from jax.experimental import pallas as pl
from jax.experimental.pallas import tpu as pltpu
from jax.sharding import PartitionSpec as P

EPS = 1e-5
MESH = pl.DeviceIdType.MESH
ROWS = 32
WIDE = 256
CHUNK = 128


def _kernel(x_hbm, g_ref, w1_hbm, w2_hbm, y_ref, w1v, w2v, inbuf, hbuf, acc, abuf, up, over,
            xsem, lsem, rsem, ssem, fsem, usem, ovsem, oss, dss, zrsem, zssem, *, S):
    s = lax.axis_index('stage')
    tp = lax.axis_index('tp')
    c = tp % 2
    sib = tp + 1 - 2 * c
    nbr = (tp + 2 - 4 * ((tp // 2) % 2), tp + 4 - 8 * (tp // 4))
    NB, _, _, D, U = w1v.shape
    R = inbuf.shape[0]
    LW = [(l, w) for w in range(2) for l in range(2)]

    def slot(b, j, k, w):
        if w == 0:
            return w1v.at[b, j, k]
        return w2v.at[b, j, pl.ds(pl.multiple_of(k * U, U), U)]

    def load(b, q, w):
        src = w1_hbm.at[0, b, :, pl.ds(q * U, U)] if w == 0 else w2_hbm.at[0, b, pl.ds(q * U, U)]
        return pltpu.make_async_copy(src, slot(b, 0, 2 * c + q, w), lsem.at[b, q, w])

    def remote(src, dst, ssem_, rsem_, stage, to):
        return pltpu.make_async_remote_copy(src_ref=src, dst_ref=dst, send_sem=ssem_, recv_sem=rsem_,
                                            device_id=(stage, to), device_id_type=MESH)

    def send(b, j, l, w):
        src = (slot(b, 0, 2 * c + l, w), slot(b, 0, 2 * c + 1 - l, w), slot(b, 1, 2 * c + 1 - l, w))[j - 1]
        return remote(src, slot(b, j, 2 * c + l, w), ssem.at[b, j - 1, l, w], rsem.at[b, j, 2 * c + l, w], s, nbr[l])

    def share(b, j, l, w):
        u = slot(b, j, 2 * c + l, w)
        return remote(u, u, fsem.at[b, j, l, w], rsem.at[b, j, 2 * c + l, w], s, sib)

    def arrived(b, j, k, w):
        u = slot(b, j, k, w)
        remote(u, u, fsem.at[b, j, 0, w], rsem.at[b, j, k, w], s, sib).wait_recv()

    helped, helper = s < S - 1, s > 0

    def go_up(l):
        return remote(slot(1, 0, 2 * c + 1 - l, 0), up.at[l], ssem.at[1, 1, l, 0], usem.at[l], s + 1, tp)

    def go_over(l):
        return remote(up.at[l], over.at[l], oss.at[l], ovsem.at[l], s, nbr[l])

    def go_down(l):
        return remote(over.at[l], slot(1, 2, 2 * c + l, 0), dss.at[l], rsem.at[1, 2, 2 * c + l, 0], s - 1, tp)

    def rows_of(i):
        return pl.ds(pl.multiple_of(i * CHUNK, CHUNK), CHUNK)

    def zsend(i):
        r = rows_of(i)
        return remote(y_ref.at[r], inbuf.at[r], zssem.at[i], zrsem.at[i], s + 1, tp)

    def each(n, body):
        def step(i, carry):
            body(i)
            return carry
        lax.fori_loop(0, n, step, 0)

    xin = pltpu.make_async_copy(x_hbm, inbuf, xsem)
    for b in range(NB):
        for q in range(2):
            for w in range(2):
                load(b, q, w).start()

    @pl.when(s == 0)
    def _():
        xin.start()

    barrier = pltpu.get_barrier_semaphore()
    for to in (sib, *nbr):
        pl.semaphore_signal(barrier, inc=1, device_id=(s, to), device_id_type=MESH)

    @pl.when(s > 0)
    def _():
        pl.semaphore_signal(barrier, inc=1, device_id=(s - 1, tp), device_id_type=MESH)

    @pl.when(s < S - 1)
    def _():
        pl.semaphore_signal(barrier, inc=1, device_id=(s + 1, tp), device_id_type=MESH)
    edge = (s == 0) | (s == S - 1)

    @pl.when(edge)
    def _():
        pl.semaphore_wait(barrier, 4)

    @pl.when(jnp.logical_not(edge))
    def _():
        pl.semaphore_wait(barrier, 5)

    for l, w in LW:
        load(0, l, w).wait()
    for j in (1, 2):
        for l, w in LW:
            send(0, j, l, w).start()
    for l, w in LW:
        load(1, l, w).wait()

    @pl.when(helped)
    def _():
        for l in range(2):
            go_up(l).start()
    for b in range(NB):
        for l, w in LW:
            share(b, 0, l, w).start()

    def own_next():
        for l, w in LW:
            send(1, 1, l, w).start()

        @pl.when(jnp.logical_not(helped))
        def _():
            for l in range(2):
                send(1, 2, l, 0).start()
        for l in range(2):
            send(1, 2, l, 1).start()

    def relay(b, j, on):
        for l, w in LW:
            arrived(b, j, 2 * c + l, w)
            if on:
                send(b, 3, 1 - l, w).start()
            share(b, j, l, w).start()

    def others(b, j):
        for l, w in LW:
            arrived(b, j, 2 * (1 - c) + l, w)

    def norm(r0, n, b, src):
        g = g_ref[0, pl.ds(b, 1), :].astype(jnp.float32)
        for r in range(0, n, ROWS):
            rows = pl.ds(r0 + r, ROWS)
            yf = src[rows, :].astype(jnp.bfloat16).astype(jnp.float32)
            acc[rows, :] = yf
            yc = yf - jnp.mean(yf, axis=-1, keepdims=True)
            var = jnp.mean(jnp.square(yc), axis=-1, keepdims=True)
            hbuf[rows, :] = (yc * lax.rsqrt(var + EPS) * g).astype(jnp.bfloat16)

    def mlp(rows, b, j0, steps):
        h = hbuf[rows, :]
        n = steps * 4 * U
        for i in range(steps):
            for k in range(4):
                z = jnp.dot(h, w1v[b, j0 + i, k], preferred_element_type=jnp.float32)
                abuf[:rows.size, (4 * i + k) * U:(4 * i + k + 1) * U] = jax.nn.gelu(z).astype(jnp.bfloat16)
        w2 = w2v[b, j0] if steps == 1 else w2v[b, j0:j0 + steps].reshape(n, D)
        acc[rows, :] += jnp.dot(abuf[:rows.size, :n], w2, preferred_element_type=jnp.float32)

    def finish(i):
        rows = rows_of(i)
        y_ref[rows, :] = acc[rows, :].astype(jnp.bfloat16)

        @pl.when(s < S - 1)
        def _():
            zsend(i).start()

    @pl.when(s == 0)
    def _():
        xin.wait()
        each(R // WIDE, lambda i: norm(pl.multiple_of(i * WIDE, WIDE), WIDE, 0, inbuf))

        def events(b, j):
            if j:
                relay(b, j, j == 1)
            if (b, j) == (0, 2):
                own_next()
            others(b, j)

        def step(t):
            b, j = t // 4, t % 4
            for e in range(4 * NB - 1):
                @pl.when(t == e)
                def _(e=e):
                    events(e // 4, e % 4)

            each(R // WIDE, lambda i: mlp(pl.ds(pl.multiple_of(i * WIDE, WIDE), WIDE), b, j, 1))

            @pl.when(t == 3)
            def _():
                each(R // WIDE, lambda i: norm(pl.multiple_of(i * WIDE, WIDE), WIDE, 1, acc))
        each(4 * NB - 1, step)
        events(NB - 1, 3)

        def last(i):
            mlp(rows_of(i), NB - 1, 3, 1)
            finish(i)
        each(R // CHUNK, last)

    @pl.when(s > 0)
    def _():
        relay(0, 1, False)
        for l in range(2):
            go_up(l).wait_recv()
            go_over(l).start()
        for l, w in LW:
            send(0, 3, l, w).start()
        relay(0, 2, False)
        own_next()
        for l in range(2):
            go_over(l).wait_recv()
            go_down(l).start()
        relay(0, 3, False)
        relay(1, 1, True)
        relay(1, 2, False)
        relay(1, 3, False)
        for b in range(NB):
            for j in range(4):
                others(b, j)

        def body(i):
            zsend(i).wait_recv()
            rows = rows_of(i)
            for b in range(NB):
                norm(rows.start, CHUNK, b, inbuf if b == 0 else acc)
                mlp(rows, b, 0, 4)
            finish(i)
        each(R // CHUNK, body)

    for b in range(NB):
        for j in range(4):
            for l, w in LW:
                share(b, j, l, w).wait_send()
                if j:
                    send(b, j, l, w).wait_send()

    @pl.when(helper)
    def _():
        for l in range(2):
            go_over(l).wait_send()
            go_down(l).wait_send()

    @pl.when(s < S - 1)
    def _():
        each(R // CHUNK, lambda i: zsend(i).wait_send())


def solution(mesh):
    S = mesh.shape['stage']

    def local(x, g, w1, w2):
        M, T, D = x.shape
        R = M * T
        n = R // CHUNK
        NB, F = w1.shape[1], w1.shape[3]
        U = F // 2
        bf, f32 = jnp.bfloat16, jnp.float32
        dma = pltpu.SemaphoreType.DMA
        y = pl.pallas_call(
            functools.partial(_kernel, S=S),
            out_shape=pltpu.VMEM((R, D), bf),
            in_specs=[pl.BlockSpec(memory_space=pl.ANY), pl.BlockSpec(memory_space=pltpu.VMEM),
                      pl.BlockSpec(memory_space=pl.ANY), pl.BlockSpec(memory_space=pl.ANY)],
            out_specs=pl.BlockSpec(memory_space=pltpu.VMEM),
            scratch_shapes=[
                pltpu.VMEM((NB, 4, 4, D, U), bf), pltpu.VMEM((NB, 4, 4 * U, D), bf),
                pltpu.VMEM((R, D), bf), pltpu.VMEM((R, D), bf),
                pltpu.VMEM((R, D), f32), pltpu.VMEM((WIDE, 16 * U), bf),
                pltpu.VMEM((2, D, U), bf), pltpu.VMEM((2, D, U), bf),
                dma(()), dma((NB, 2, 2)), dma((NB, 4, 4, 2)), dma((NB, 3, 2, 2)), dma((NB, 4, 2, 2)),
                dma((2,)), dma((2,)), dma((2,)), dma((2,)),
                dma((n,)), dma((n,)),
            ],
            compiler_params=pltpu.CompilerParams(
                collective_id=0, has_side_effects=True, vmem_limit_bytes=62 * 1000 * 1000),
        )(x.reshape(R, D), g, w1, w2)
        return y.reshape(1, M, T, D)

    return jax.shard_map(
        local, mesh=mesh,
        in_specs=(P(None, 'tp', None), P('stage', None, None),
                  P('stage', None, None, 'tp'), P('stage', None, 'tp', None)),
        out_specs=P('stage', None, 'tp', None), check_vma=False)
```

time: 270 us -> 263 us (0.974)
  Pallas kernels: 265 us -> 261 us
    pallas_call x1, Pallas kernels: 265 us -> 261 us  [local(): pl.pallas_call(functools.partial(_kernel, S=S), out_shape=pltpu.VMEM((R,...]
where the time goes in v6:
time: 263 us
  Pallas kernels  261 us (99%)
    pallas_call x1, Pallas kernels, local(): pl.pallas_call(functools.partial(_kernel, S=S), out_shape=pltpu.VMEM((R,...  261 us

profile of v6, /device:TPU:24, one launch (start us, length us, event | category | flops | bytes accessed | tf_op | source)
XLA Modules:
  0.0 262.6 jit_solution(8938567650980320337)
XLA Ops:
  0.0 260.6 %shard_map.46 = bf16[2048,1024]{1,0:T(8,128)(2,1)S(1)} custom-call(bf16[2048,1024]{1,0:T(8,128)(2,1)} %bitcast.3, bf16[1,2,1024]{2,1,0:T(2,128)(2,1)} %g_ref.1, bf16[1,2,1024,512]{3,2,1,0:T(8,128)(2,1)} %w1_hbm.1, bf16[1,2,512,1024]{3,2,1,0:T(8,128)(2,1)} %w2_hbm.1), custom_call_target="tpu_custom_call" | custom-call | tf_op jit(solution)/shard_map/pallas_call | solution.py:265
  260.6 2.0 copy.6

commit v7 on v6

--- a/solution.py
+++ b/solution.py
@@ -12,9 +12,10 @@
 ROWS = 32
 WIDE = 256
 CHUNK = 128
-
-
-def _kernel(x_hbm, g_ref, w1_hbm, w2_hbm, y_ref, w1v, w2v, inbuf, hbuf, acc, abuf, up, over,
+LAG = 4
+
+
+def _kernel(x_hbm, g_ref, w1_hbm, w2_hbm, y_ref, w1v, w2v, inbuf, hbuf, acc, abuf, up0, up1, up2, over0, over1, over2,
             xsem, lsem, rsem, ssem, fsem, usem, ovsem, oss, dss, zrsem, zssem, *, S):
     s = lax.axis_index('stage')
     tp = lax.axis_index('tp')
@@ -23,15 +24,17 @@
     nbr = (tp + 2 - 4 * ((tp // 2) % 2), tp + 4 - 8 * (tp // 4))
     NB, _, _, D, U = w1v.shape
     R = inbuf.shape[0]
-    LW = [(l, w) for w in range(2) for l in range(2)]
+    LW = [(l, w) for w in range(3) for l in range(2)]
+    H = U // 2
+    up, over = (up0, up1, up2), (over0, over1, over2)
 
     def slot(b, j, k, w):
         if w == 0:
             return w1v.at[b, j, k]
-        return w2v.at[b, j, pl.ds(pl.multiple_of(k * U, U), U)]
+        return w2v.at[b, j, pl.ds(pl.multiple_of(k * U + (w - 1) * H, H), H)]
 
     def load(b, q, w):
-        src = w1_hbm.at[0, b, :, pl.ds(q * U, U)] if w == 0 else w2_hbm.at[0, b, pl.ds(q * U, U)]
+        src = w1_hbm.at[0, b, :, pl.ds(q * U, U)] if w == 0 else w2_hbm.at[0, b, pl.ds(q * U + (w - 1) * H, H)]
         return pltpu.make_async_copy(src, slot(b, 0, 2 * c + q, w), lsem.at[b, q, w])
 
     def remote(src, dst, ssem_, rsem_, stage, to):
@@ -50,16 +53,27 @@
         u = slot(b, j, k, w)
         remote(u, u, fsem.at[b, j, 0, w], rsem.at[b, j, k, w], s, sib).wait_recv()
 
-    helped, helper = s < S - 1, s > 0
-
-    def go_up(l):
-        return remote(slot(1, 0, 2 * c + 1 - l, 0), up.at[l], ssem.at[1, 1, l, 0], usem.at[l], s + 1, tp)
-
-    def go_over(l):
-        return remote(up.at[l], over.at[l], oss.at[l], ovsem.at[l], s, nbr[l])
-
-    def go_down(l):
-        return remote(over.at[l], slot(1, 2, 2 * c + l, 0), dss.at[l], rsem.at[1, 2, 2 * c + l, 0], s - 1, tp)
+    def helped(w):
+        return (s < S - 1) if w < 2 else (s == 1)
+
+    def helper(w):
+        return (s > 0) if w < 2 else (s == 2)
+
+    def go_up(l, w):
+        return remote(slot(1, 0, 2 * c + 1 - l, w), up[w].at[l], ssem.at[1, 1, l, w], usem.at[l, w], s + 1, tp)
+
+    def go_over(l, w):
+        return remote(up[w].at[l], over[w].at[l], oss.at[l, w], ovsem.at[l, w], s, nbr[l])
+
+    def go_down(l, w):
+        return remote(over[w].at[l], slot(1, 2, 2 * c + l, w), dss.at[l, w], rsem.at[1, 2, 2 * c + l, w], s - 1, tp)
+
+    def each_part(cond, body):
+        for w in range(3):
+            @pl.when(cond(w))
+            def _(w=w):
+                for l in range(2):
+                    body(l, w)
 
     def rows_of(i):
         return pl.ds(pl.multiple_of(i * CHUNK, CHUNK), CHUNK)
@@ -76,9 +90,8 @@
 
     xin = pltpu.make_async_copy(x_hbm, inbuf, xsem)
     for b in range(NB):
-        for q in range(2):
-            for w in range(2):
-                load(b, q, w).start()
+        for q, w in LW:
+            load(b, q, w).start()
 
     @pl.when(s == 0)
     def _():
@@ -112,11 +125,7 @@
             send(0, j, l, w).start()
     for l, w in LW:
         load(1, l, w).wait()
-
-    @pl.when(helped)
-    def _():
-        for l in range(2):
-            go_up(l).start()
+    each_part(helped, lambda l, w: go_up(l, w).start())
     for b in range(NB):
         for l, w in LW:
             share(b, 0, l, w).start()
@@ -125,12 +134,7 @@
         for l, w in LW:
             send(1, 1, l, w).start()
 
-        @pl.when(jnp.logical_not(helped))
-        def _():
-            for l in range(2):
-                send(1, 2, l, 0).start()
-        for l in range(2):
-            send(1, 2, l, 1).start()
+        each_part(lambda w: jnp.logical_not(helped(w)), lambda l, w: send(1, 2, l, w).start())
 
     def relay(b, j, on):
         for l, w in LW:
@@ -167,10 +171,6 @@
         rows = rows_of(i)
         y_ref[rows, :] = acc[rows, :].astype(jnp.bfloat16)
 
-        @pl.when(s < S - 1)
-        def _():
-            zsend(i).start()
-
     @pl.when(s == 0)
     def _():
         xin.wait()
@@ -198,24 +198,37 @@
         each(4 * NB - 1, step)
         events(NB - 1, 3)
 
+        lag = LAG * c
+
         def last(i):
             mlp(rows_of(i), NB - 1, 3, 1)
             finish(i)
+
+            @pl.when(i >= lag)
+            def _():
+                zsend(i - lag).start()
         each(R // CHUNK, last)
 
+        @pl.when(c == 1)
+        def _():
+            each(LAG, lambda i: zsend(R // CHUNK - LAG + i).start())
+
     @pl.when(s > 0)
     def _():
         relay(0, 1, False)
-        for l in range(2):
-            go_up(l).wait_recv()
-            go_over(l).start()
+        def over_(l, w):
+            go_up(l, w).wait_recv()
+            go_over(l, w).start()
+
+        def down_(l, w):
+            go_over(l, w).wait_recv()
+            go_down(l, w).start()
+        each_part(helper, over_)
         for l, w in LW:
             send(0, 3, l, w).start()
         relay(0, 2, False)
         own_next()
-        for l in range(2):
-            go_over(l).wait_recv()
-            go_down(l).start()
+        each_part(helper, down_)
         relay(0, 3, False)
         relay(1, 1, True)
         relay(1, 2, False)
@@ -231,6 +244,10 @@
                 norm(rows.start, CHUNK, b, inbuf if b == 0 else acc)
                 mlp(rows, b, 0, 4)
             finish(i)
+
+            @pl.when(s < S - 1)
+            def _():
+                zsend(i).start()
         each(R // CHUNK, body)
 
     for b in range(NB):
@@ -240,11 +257,10 @@
                 if j:
                     send(b, j, l, w).wait_send()
 
-    @pl.when(helper)
-    def _():
-        for l in range(2):
-            go_over(l).wait_send()
-            go_down(l).wait_send()
+    def helped_on(l, w):
+        go_over(l, w).wait_send()
+        go_down(l, w).wait_send()
+    each_part(helper, helped_on)
 
     @pl.when(s < S - 1)
     def _():
@@ -272,9 +288,9 @@
                 pltpu.VMEM((NB, 4, 4, D, U), bf), pltpu.VMEM((NB, 4, 4 * U, D), bf),
                 pltpu.VMEM((R, D), bf), pltpu.VMEM((R, D), bf),
                 pltpu.VMEM((R, D), f32), pltpu.VMEM((WIDE, 16 * U), bf),
-                pltpu.VMEM((2, D, U), bf), pltpu.VMEM((2, D, U), bf),
-                dma(()), dma((NB, 2, 2)), dma((NB, 4, 4, 2)), dma((NB, 3, 2, 2)), dma((NB, 4, 2, 2)),
-                dma((2,)), dma((2,)), dma((2,)), dma((2,)),
+                *([pltpu.VMEM((2, D, U), bf)] + [pltpu.VMEM((2, U // 2, D), bf)] * 2) * 2,
+                dma(()), dma((NB, 2, 3)), dma((NB, 4, 4, 3)), dma((NB, 3, 2, 3)), dma((NB, 4, 2, 3)),
+                dma((2, 3)), dma((2, 3)), dma((2, 3)), dma((2, 3)),
                 dma((n,)), dma((n,)),
             ],
             compiler_params=pltpu.CompilerParams(

time: 263 us -> 260 us (0.989)
  Pallas kernels: 261 us -> 257 us
    pallas_call x1, Pallas kernels: 261 us -> 257 us  [local(): pl.pallas_call(functools.partial(_kernel, S=S), out_shape=pltpu.VMEM((R,...]
where the time goes in v7:
time: 260 us; the launch traced here: 259 us
  Pallas kernels  257 us (99%)
    pallas_call x1, Pallas kernels, local(): pl.pallas_call(functools.partial(_kernel, S=S), out_shape=pltpu.VMEM((R,...  257 us

profile of v7, /device:TPU:24, one launch (start us, length us, event | category | flops | bytes accessed | tf_op | source)
XLA Modules:
  0.0 258.9 jit_solution(9108100040667392412)
XLA Ops:
  0.0 256.9 %shard_map.46 = bf16[2048,1024]{1,0:T(8,128)(2,1)S(1)} custom-call(bf16[2048,1024]{1,0:T(8,128)(2,1)} %bitcast.3, bf16[1,2,1024]{2,1,0:T(2,128)(2,1)} %g_ref.1, bf16[1,2,1024,512]{3,2,1,0:T(8,128)(2,1)} %w1_hbm.1, bf16[1,2,512,1024]{3,2,1,0:T(8,128)(2,1)} %w2_hbm.1), custom_call_target="tpu_custom_call" | custom-call | tf_op jit(solution)/shard_map/pallas_call | solution.py:281
  256.9 2.0 copy.6

commit v8 on v7

--- a/solution.py
+++ b/solution.py
@@ -142,6 +142,8 @@
             if on:
                 send(b, 3, 1 - l, w).start()
             share(b, j, l, w).start()
+            if (b, j, l, w) == (0, 3, 1, 0):
+                own_next()
 
     def others(b, j):
         for l, w in LW:
@@ -179,8 +181,6 @@
         def events(b, j):
             if j:
                 relay(b, j, j == 1)
-            if (b, j) == (0, 2):
-                own_next()
             others(b, j)
 
         def step(t):
@@ -227,7 +227,6 @@
         for l, w in LW:
             send(0, 3, l, w).start()
         relay(0, 2, False)
-        own_next()
         each_part(helper, down_)
         relay(0, 3, False)
         relay(1, 1, True)

time: 260 us -> 260 us (level)
  no operation moved by 1% of the time
where the time goes in v8:
time: 260 us; the launch traced here: 258 us
  Pallas kernels  256 us (98%)
    pallas_call x1, Pallas kernels, local(): pl.pallas_call(functools.partial(_kernel, S=S), out_shape=pltpu.VMEM((R,...  256 us

profile of v8, /device:TPU:24, one launch (start us, length us, event | category | flops | bytes accessed | tf_op | source)
XLA Modules:
  0.0 258.3 jit_solution(8550018894085480621)
XLA Ops:
  0.0 256.3 %shard_map.46 = bf16[2048,1024]{1,0:T(8,128)(2,1)S(1)} custom-call(bf16[2048,1024]{1,0:T(8,128)(2,1)} %bitcast.3, bf16[1,2,1024]{2,1,0:T(2,128)(2,1)} %g_ref.1, bf16[1,2,1024,512]{3,2,1,0:T(8,128)(2,1)} %w1_hbm.1, bf16[1,2,512,1024]{3,2,1,0:T(8,128)(2,1)} %w2_hbm.1), custom_call_target="tpu_custom_call" | custom-call | tf_op jit(solution)/shard_map/pallas_call | solution.py:280
  256.3 2.0 copy.6

commit v9 on v8

--- a/solution.py
+++ b/solution.py
@@ -179,7 +179,7 @@
         each(R // WIDE, lambda i: norm(pl.multiple_of(i * WIDE, WIDE), WIDE, 0, inbuf))
 
         def events(b, j):
-            if j:
+            if j and (b, j) != (1, 1):
                 relay(b, j, j == 1)
             others(b, j)
 
@@ -190,7 +190,12 @@
                 def _(e=e):
                     events(e // 4, e % 4)
 
-            each(R // WIDE, lambda i: mlp(pl.ds(pl.multiple_of(i * WIDE, WIDE), WIDE), b, j, 1))
+            def wide(i):
+                @pl.when((t == 4) & (i == R // WIDE // 2))
+                def _():
+                    relay(1, 1, True)
+                mlp(pl.ds(pl.multiple_of(i * WIDE, WIDE), WIDE), b, j, 1)
+            each(R // WIDE, wide)
 
             @pl.when(t == 3)
             def _():

time: 260 us -> 260 us (level)
  no operation moved by 1% of the time
where the time goes in v9:
time: 260 us; the launch traced here: 256 us
  Pallas kernels  254 us (98%)
    pallas_call x1, Pallas kernels, local(): pl.pallas_call(functools.partial(_kernel, S=S), out_shape=pltpu.VMEM((R,...  254 us

profile of v9, /device:TPU:24, one launch (start us, length us, event | category | flops | bytes accessed | tf_op | source)
XLA Modules:
  0.0 256.2 jit_solution(3765556553495906403)
XLA Ops:
  0.0 254.2 %shard_map.46 = bf16[2048,1024]{1,0:T(8,128)(2,1)S(1)} custom-call(bf16[2048,1024]{1,0:T(8,128)(2,1)} %bitcast.3, bf16[1,2,1024]{2,1,0:T(2,128)(2,1)} %g_ref.1, bf16[1,2,1024,512]{3,2,1,0:T(8,128)(2,1)} %w1_hbm.1, bf16[1,2,512,1024]{3,2,1,0:T(8,128)(2,1)} %w2_hbm.1), custom_call_target="tpu_custom_call" | custom-call | tf_op jit(solution)/shard_map/pallas_call | solution.py:285
  254.2 2.0 copy.6

commit v10 on v9

--- a/solution.py
+++ b/solution.py
@@ -12,7 +12,7 @@
 ROWS = 32
 WIDE = 256
 CHUNK = 128
-LAG = 4
+LAG = 2
 
 
 def _kernel(x_hbm, g_ref, w1_hbm, w2_hbm, y_ref, w1v, w2v, inbuf, hbuf, acc, abuf, up0, up1, up2, over0, over1, over2,

time: 260 us -> 259 us (level); the launches traced: 256 us -> 258 us
  no operation moved by 1% of the time
where the time goes in v10:
time: 259 us; the launch traced here: 258 us
  Pallas kernels  256 us (99%)
    pallas_call x1, Pallas kernels, local(): pl.pallas_call(functools.partial(_kernel, S=S), out_shape=pltpu.VMEM((R,...  256 us

profile of v10, /device:TPU:24, one launch (start us, length us, event | category | flops | bytes accessed | tf_op | source)
XLA Modules:
  0.0 258.0 jit_solution(6319668428034371919)
XLA Ops:
  0.0 256.0 %shard_map.46 = bf16[2048,1024]{1,0:T(8,128)(2,1)S(1)} custom-call(bf16[2048,1024]{1,0:T(8,128)(2,1)} %bitcast.3, bf16[1,2,1024]{2,1,0:T(2,128)(2,1)} %g_ref.1, bf16[1,2,1024,512]{3,2,1,0:T(8,128)(2,1)} %w1_hbm.1, bf16[1,2,512,1024]{3,2,1,0:T(8,128)(2,1)} %w2_hbm.1), custom_call_target="tpu_custom_call" | custom-call | tf_op jit(solution)/shard_map/pallas_call | solution.py:285
  256.0 2.0 copy.6

commit v11 on v10

--- a/solution.py
+++ b/solution.py
@@ -159,7 +159,7 @@
             var = jnp.mean(jnp.square(yc), axis=-1, keepdims=True)
             hbuf[rows, :] = (yc * lax.rsqrt(var + EPS) * g).astype(jnp.bfloat16)
 
-    def mlp(rows, b, j0, steps):
+    def mlp(rows, b, j0, steps, final=False):
         h = hbuf[rows, :]
         n = steps * 4 * U
         for i in range(steps):
@@ -167,11 +167,11 @@
                 z = jnp.dot(h, w1v[b, j0 + i, k], preferred_element_type=jnp.float32)
                 abuf[:rows.size, (4 * i + k) * U:(4 * i + k + 1) * U] = jax.nn.gelu(z).astype(jnp.bfloat16)
         w2 = w2v[b, j0] if steps == 1 else w2v[b, j0:j0 + steps].reshape(n, D)
-        acc[rows, :] += jnp.dot(abuf[:rows.size, :n], w2, preferred_element_type=jnp.float32)
-
-    def finish(i):
-        rows = rows_of(i)
-        y_ref[rows, :] = acc[rows, :].astype(jnp.bfloat16)
+        total = acc[rows, :] + jnp.dot(abuf[:rows.size, :n], w2, preferred_element_type=jnp.float32)
+        if final:
+            y_ref[rows, :] = total.astype(jnp.bfloat16)
+        else:
+            acc[rows, :] = total
 
     @pl.when(s == 0)
     def _():
@@ -206,8 +206,7 @@
         lag = LAG * c
 
         def last(i):
-            mlp(rows_of(i), NB - 1, 3, 1)
-            finish(i)
+            mlp(rows_of(i), NB - 1, 3, 1, final=True)
 
             @pl.when(i >= lag)
             def _():
@@ -246,8 +245,7 @@
             rows = rows_of(i)
             for b in range(NB):
                 norm(rows.start, CHUNK, b, inbuf if b == 0 else acc)
-                mlp(rows, b, 0, 4)
-            finish(i)
+                mlp(rows, b, 0, 4, final=b == NB - 1)
 
             @pl.when(s < S - 1)
             def _():

time: 259 us -> 259 us (level)
  no operation moved by 1% of the time
where the time goes in v11:
time: 259 us; the launch traced here: 258 us
  Pallas kernels  256 us (99%)
    pallas_call x1, Pallas kernels, local(): pl.pallas_call(functools.partial(_kernel, S=S), out_shape=pltpu.VMEM((R,...  256 us

profile of v11, /device:TPU:24, one launch (start us, length us, event | category | flops | bytes accessed | tf_op | source)
XLA Modules:
  0.0 258.0 jit_solution(15714091581087785513)
XLA Ops:
  0.0 256.0 %shard_map.46 = bf16[2048,1024]{1,0:T(8,128)(2,1)S(1)} custom-call(bf16[2048,1024]{1,0:T(8,128)(2,1)} %bitcast.3, bf16[1,2,1024]{2,1,0:T(2,128)(2,1)} %g_ref.1, bf16[1,2,1024,512]{3,2,1,0:T(8,128)(2,1)} %w1_hbm.1, bf16[1,2,512,1024]{3,2,1,0:T(8,128)(2,1)} %w2_hbm.1), custom_call_target="tpu_custom_call" | custom-call | tf_op jit(solution)/shard_map/pallas_call | solution.py:283
  256.0 2.0 copy.6
